TPU v7x, 16 devices: a whole 2x2x2 slice. The times are simulated.
16 devices in a mesh: dpy: 2 (over z), dpx: 2 (over y), tp: 4 (over x, core).
Axes of the slice: x: 2, y: 2, z: 2, core: 2. Of those that a mesh axis runs over, the one named last changes fastest.
Arguments:
- x_saved: bfloat16 [2, 64, 512, 768], P(None, ('dpy', 'dpx'))
- y_saved: bfloat16 [2, 64, 512, 768], P(None, ('dpy', 'dpx'))
- dz_top: bfloat16 [64, 512, 768], P(('dpy', 'dpx'))
- w_qkv: bfloat16 [2, 768, 3, 12, 64], P(None, None, None, 'tp')
- w_out: bfloat16 [2, 12, 64, 768], P(None, 'tp')
- w_up: bfloat16 [2, 768, 3072], P(None, None, 'tp')
- w_down: bfloat16 [2, 3072, 768], P(None, 'tp')
Outputs:
- output 1: bfloat16 [64, 512, 768], P(('dpy', 'dpx'))
- output 2: float32 [2, 768, 3, 12, 64], P(None, ('dpy', 'dpx'), None, 'tp')
- output 3: float32 [2, 12, 64, 768], P(None, 'tp', None, ('dpy', 'dpx'))
- output 4: float32 [2, 768, 3072], P(None, ('dpy', 'dpx'), 'tp')
- output 5: float32 [2, 3072, 768], P(None, ('tp', 'dpy', 'dpx'))
All inputs are finite; a program needn't handle non-finite values.
Results may differ from a plain program's by a relative error of at most 0.0179834.
Values are sent between devices in bfloat16 or wider.
A program may use at most 1 GiB of HBM per device.

v0:
```python
import jax
import jax.numpy as jnp
from jax import lax
from jax.sharding import PartitionSpec as P

DATA_AXES = ('dpy', 'dpx')


def layer_backward(x_in, y_mid, d_out, w_qkv, w_out, w_up, w_down):
    head_dim = w_qkv.shape[-1]
    attn_scale = head_dim ** -0.5
    h_pre = jnp.einsum('bsd,df->bsf', y_mid, w_up, preferred_element_type=jnp.float32)
    gelu_out, gelu_pull = jax.vjp(jax.nn.gelu, h_pre)
    gelu_bf = gelu_out.astype(jnp.bfloat16)
    g_down = jnp.einsum('bsf,bsd->fd', gelu_bf, d_out, preferred_element_type=jnp.float32)
    d_gelu = jnp.einsum('bsd,fd->bsf', d_out, w_down, preferred_element_type=jnp.float32)
    d_pre = gelu_pull(d_gelu)[0].astype(jnp.bfloat16)
    g_up = jnp.einsum('bsd,bsf->df', y_mid, d_pre, preferred_element_type=jnp.float32)
    mlp_part = jnp.einsum('bsf,df->bsd', d_pre, w_up, preferred_element_type=jnp.float32)
    d_mid = (d_out.astype(jnp.float32) + lax.psum(mlp_part, 'tp')).astype(jnp.bfloat16)
    qkv_act = jnp.einsum('bsd,dche->bsche', x_in, w_qkv, preferred_element_type=jnp.float32).astype(jnp.bfloat16)
    q_heads = qkv_act[:, :, 0]
    k_heads = qkv_act[:, :, 1]
    v_heads = qkv_act[:, :, 2]
    scores = jnp.einsum('bqhe,bkhe->bhqk', q_heads, k_heads, preferred_element_type=jnp.float32) * attn_scale
    attn_prob = jax.nn.softmax(scores, axis=-1)
    prob_bf = attn_prob.astype(jnp.bfloat16)
    context = jnp.einsum('bhqk,bkhe->bqhe', prob_bf, v_heads, preferred_element_type=jnp.float32).astype(jnp.bfloat16)
    g_out = jnp.einsum('crif,cre->ife', context, d_mid, preferred_element_type=jnp.float32)
    d_ctx = jnp.einsum('cre,ife->crif', d_mid, w_out, preferred_element_type=jnp.float32).astype(jnp.bfloat16)
    d_prob = jnp.einsum('bqhe,bkhe->bhqk', d_ctx, v_heads, preferred_element_type=jnp.float32)
    d_val = jnp.einsum('bhqk,bqhe->bkhe', prob_bf, d_ctx, preferred_element_type=jnp.float32).astype(jnp.bfloat16)
    row_dot = jnp.sum(d_prob * attn_prob, axis=-1, keepdims=True)
    d_scores = (attn_prob * (d_prob - row_dot) * attn_scale).astype(jnp.bfloat16)
    d_query = jnp.einsum('bhqk,bkhe->bqhe', d_scores, k_heads, preferred_element_type=jnp.float32).astype(jnp.bfloat16)
    d_key = jnp.einsum('bhqk,bqhe->bkhe', d_scores, q_heads, preferred_element_type=jnp.float32).astype(jnp.bfloat16)
    d_qkv = jnp.stack([d_query, d_key, d_val], axis=2)
    g_qkv = jnp.einsum('bsd,bsche->dche', x_in, d_qkv, preferred_element_type=jnp.float32)
    attn_part = jnp.einsum('bsche,dche->bsd', d_qkv, w_qkv, preferred_element_type=jnp.float32)
    d_input = (d_mid.astype(jnp.float32) + lax.psum(attn_part, 'tp')).astype(jnp.bfloat16)
    return d_input, (g_qkv, g_out, g_up, g_down)


def reduce_grads(local_grad, replicas):
    g_qkv, g_out, g_up, g_down = local_grad
    return (lax.psum_scatter(g_qkv, DATA_AXES, scatter_dimension=0, tiled=True) / replicas,
            lax.psum_scatter(g_out, DATA_AXES, scatter_dimension=2, tiled=True) / replicas,
            lax.psum_scatter(g_up, DATA_AXES, scatter_dimension=0, tiled=True) / replicas,
            lax.psum_scatter(g_down, DATA_AXES, scatter_dimension=0, tiled=True) / replicas)


def solution(mesh):
    replicas = mesh.shape['dpy'] * mesh.shape['dpx']
    act_spec = P(None, DATA_AXES, None, None)

    def device_backward(x_saved, y_saved, dz_top, w_qkv, w_out, w_up, w_down):
        grad_in = dz_top
        reduced = []
        for layer_idx in reversed(range(x_saved.shape[0])):
            grad_in, local_grad = layer_backward(x_saved[layer_idx], y_saved[layer_idx], grad_in, w_qkv[layer_idx], w_out[layer_idx], w_up[layer_idx], w_down[layer_idx])
            reduced.insert(0, reduce_grads(local_grad, replicas))
        stacked = tuple(jnp.stack([layer_grad[slot_idx] for layer_grad in reduced]) for slot_idx in range(4))
        return (grad_in,) + stacked

    return jax.shard_map(device_backward, mesh=mesh,
                         in_specs=(act_spec, act_spec, P(DATA_AXES, None, None), P(None, None, None, 'tp', None), P(None, 'tp', None, None), P(None, None, 'tp'), P(None, 'tp', None)),
                         out_specs=(P(DATA_AXES, None, None), P(None, DATA_AXES, None, 'tp', None), P(None, 'tp', None, DATA_AXES), P(None, DATA_AXES, 'tp'), P(None, ('tp', 'dpy', 'dpx'), None)),
                         check_vma=False)
```

profile of v0, /device:TPU:0, one launch (start us, length us, event | category | flops | bytes accessed | tf_op | source)
XLA Modules:
  0.0 2298.8 jit_solution(16146784620116798069)
XLA Ops:
  8.1 17.9 fusion.74
  26.0 28.7 %fusion.22 = bf16[16,512,768]{2,1,0:T(8,128)(2,1)} fusion(f32[16,512,768]{2,1,0:T(8,128)} %fusion.74, bf16[16,512,768]{2,1,0:T(8,128)(2,1)} %param.9, bf16[2,768,768]{2,1,0:T(8,128)(2,1)S(1)} %copy-done.9), kind=kOutput, calls=%fused_computation.26 | convolution fusion | flops 9789505536 | bytes 51511296 | tf_op jit(solution)/shard_map/bsd,fd->bsf/dot_general | solution.py:16
  54.7 18.7 fusion.161
  73.5 1.4 copy-done.14
  74.9 14.5 fusion.86
  89.4 25.0 %fusion.214 = (f32[16,3,512]{2,1,0:T(4,128)S(1)}, f32[16,3,512,512]{2,3,1,0:T(8,128)}) fusion(bf16[16,512,3,3,64]{1,4,3,2,0:T(8,128)(2,1)} %fusion.86), kind=kOutput, calls=%fused_computation.188 | convolution fusion | flops 1648361984 | bytes 56721408 | tf_op jit(solution)/shard_map/sub | solution.py:26
  114.4 27.4 %fusion.212 = bf16[16,3,512,512]{2,3,1,0:T(8,128)(2,1)} fusion(f32[16,3,512,512]{2,3,1,0:T(8,128)} %get-tuple-element.16, f32[16,3,512]{2,1,0:T(4,128)S(1)} %get-tuple-element.15), kind=kLoop, calls=%fused_computation.186 | loop fusion | flops 25165824 | bytes 75595776 | tf_op jit(solution)/shard_map/convert_element_type | solution.py:27
  141.8 353.6 %all-reduce.5.cloned.1.call-done = f32[16,512,768]{2,1,0:T(8,128)} async-done(((f32[16,512,768]{2,1,0:T(8,128)}), f32[16,512,768]{2,1,0:T(8,128)}) %all-reduce.5.cloned.1.call-update) | async-done | bytes 25165840 | tf_op jit(solution)/shard_map/psum | solution.py:20
  495.4 12.8 add_convert_fusion.3
  508.2 4.4 copy-done.2
  512.7 4.4 fusion.116
  517.1 31.4 %fusion.210 = f32[16,3,512,512]{2,3,1,0:T(8,128)} fusion(bf16[16,512,3,64]{1,3,2,0:T(8,128)(2,1)S(1)} %fusion.116, bf16[16,512,3,3,64]{1,4,3,2,0:T(8,128)(2,1)} %fusion.86), kind=kOutput, calls=%fused_computation.184 | convolution fusion | flops 1610612736 | bytes 56623104 | tf_op jit(solution)/shard_map/bqhe,bkhe->bhqk/dot_general | solution.py:31
  548.5 63.8 %convert_bitcast_fusion.4 = bf16[16,512,1,3,64]{1,4,3,0,2:T(8,128)(2,1)} fusion(f32[16,3,512,512]{2,3,1,0:T(8,128)} %fusion.210, bf16[16,512,3,3,64]{1,4,3,2,0:T(8,128)(2,1)} %fusion.86, f32[16,3,512,512]{2,3,1,0:T(8,128)} %get-tuple-element.16, f32[16,3,512]{2,1,0:T(4,128)S(1)} %get-tuple-element.15), kind=kOutput, calls=%fused_computation.110 | convolution fusion | flops 1700291072 | bytes 207880192 | tf_op jit(solution)/shard_map/bhqk,bqhe->bkhe/dot_general | solution.py:36
  612.3 64.1 %convert_bitcast_fusion.5 = bf16[16,512,1,3,64]{1,4,3,0,2:T(8,128)(2,1)} fusion(f32[16,3,512,512]{2,3,1,0:T(8,128)} %fusion.210, bf16[16,512,3,3,64]{1,4,3,2,0:T(8,128)(2,1)} %fusion.86, f32[16,3,512,512]{2,3,1,0:T(8,128)} %get-tuple-element.16, f32[16,3,512]{2,1,0:T(4,128)S(1)} %get-tuple-element.15), kind=kOutput, calls=%fused_computation.111 | convolution fusion | flops 1700291072 | bytes 207880192 | tf_op jit(solution)/shard_map/bhqk,bkhe->bqhe/dot_general | solution.py:35
  676.4 13.5 convert_bitcast_fusion.3
  689.9 17.8 convolution_bitcast_fusion.1
  707.8 1.6 copy-done.12
  709.4 18.5 fusion.68
  727.9 399.2 %all-reduce.7.cloned.1.call-done = f32[16,512,768]{2,1,0:T(8,128)} async-done(((f32[16,512,768]{2,1,0:T(8,128)}), f32[16,512,768]{2,1,0:T(8,128)}) %all-reduce.7.cloned.1.call-update) | async-done | bytes 25165840 | tf_op jit(solution)/shard_map/psum | solution.py:40
  1127.1 12.8 add_convert_fusion.2
  1139.9 4.5 copy-done.1
  1144.4 26.8 %fusion.29 = bf16[16,512,768]{2,1,0:T(8,128)(2,1)} fusion(f32[16,512,768]{2,1,0:T(8,128)} %fusion.68, bf16[16,512,768]{2,1,0:T(8,128)(2,1)S(1)} %add_convert_fusion.2, bf16[2,768,768]{2,1,0:T(8,128)(2,1)S(1)} %copy-done.10), kind=kOutput, calls=%fused_computation.33 | convolution fusion | flops 9789505536 | bytes 51511296 | tf_op jit(solution)/shard_map/bsd,fd->bsf/dot_general | solution.py:16
  1171.2 18.4 fusion.156
  1189.8 19.2 fusion.130
  1209.1 14.9 fusion.132
  1224.0 2.0 copy.92
  1226.0 13.1 fusion.89
  1239.2 16.1 fusion.138
  1256.0 1.7 reshape.44
  1257.8 14.8 fusion.52
  1272.6 2.2 copy.100
  1274.8 25.0 %fusion.215 = (f32[16,3,512]{2,1,0:T(4,128)S(1)}, f32[16,3,512,512]{2,3,1,0:T(8,128)}) fusion(bf16[16,512,3,3,64]{1,4,3,2,0:T(8,128)(2,1)} %fusion.89), kind=kOutput, calls=%fused_computation.189 | convolution fusion | flops 1648361984 | bytes 56721408 | tf_op jit(solution)/shard_map/sub | solution.py:26
  1299.8 18.8 fusion.131
  1318.7 27.4 %fusion.213 = bf16[16,3,512,512]{2,3,1,0:T(8,128)(2,1)} fusion(f32[16,3,512,512]{2,3,1,0:T(8,128)} %get-tuple-element.18, f32[16,3,512]{2,1,0:T(4,128)S(1)} %get-tuple-element.17), kind=kLoop, calls=%fused_computation.187 | loop fusion | flops 25165824 | bytes 75595776 | tf_op jit(solution)/shard_map/convert_element_type | solution.py:27
  1346.1 15.0 fusion.135
  1361.1 2.0 copy.90
  1363.1 245.9 %all-reduce.9.cloned.1.call-done = f32[16,512,768]{2,1,0:T(8,128)} async-done(((f32[16,512,768]{2,1,0:T(8,128)}), f32[16,512,768]{2,1,0:T(8,128)}) %all-reduce.9.cloned.1.call-update) | async-done | bytes 25165840 | tf_op jit(solution)/shard_map/psum | solution.py:20
  1609.1 12.9 add_convert_fusion.1
  1622.0 4.8 copy-done
  1626.8 5.3 fusion.119
  1632.1 18.0 fusion.147
  1650.1 2.4 copy.86
  1652.5 2.7 reshape.42
  1655.2 21.3 fusion.211
  1676.5 63.9 %convert_bitcast_fusion.2 = bf16[16,512,1,3,64]{1,4,3,0,2:T(8,128)(2,1)} fusion(f32[16,3,512,512]{2,3,1,0:T(8,128)} %fusion.211, bf16[16,512,3,3,64]{1,4,3,2,0:T(8,128)(2,1)} %fusion.89, f32[16,3,512,512]{2,3,1,0:T(8,128)} %get-tuple-element.18, f32[16,3,512]{2,1,0:T(4,128)S(1)} %get-tuple-element.17), kind=kOutput, calls=%fused_computation.108 | convolution fusion | flops 1700291072 | bytes 207880192 | tf_op jit(solution)/shard_map/bhqk,bkhe->bqhe/dot_general | solution.py:35
  1740.3 64.2 %convert_bitcast_fusion.1 = bf16[16,512,1,3,64]{1,4,3,0,2:T(8,128)(2,1)} fusion(f32[16,3,512,512]{2,3,1,0:T(8,128)} %fusion.211, bf16[16,512,3,3,64]{1,4,3,2,0:T(8,128)(2,1)} %fusion.89, f32[16,3,512,512]{2,3,1,0:T(8,128)} %get-tuple-element.18, f32[16,3,512]{2,1,0:T(4,128)S(1)} %get-tuple-element.17), kind=kOutput, calls=%fused_computation.107 | convolution fusion | flops 1700291072 | bytes 207880192 | tf_op jit(solution)/shard_map/bhqk,bqhe->bkhe/dot_general | solution.py:36
  1804.5 13.5 convert_bitcast_fusion
  1818.1 16.1 fusion.54
  1834.2 2.9 copy.98
  1837.2 17.3 convolution_bitcast_fusion
  1854.5 1.3 copy.97
  1855.9 1.3 copy.93
  1857.4 1.1 reshape.45
  1858.7 1.2 copy.101
  1860.8 1.3 copy.95
  1862.4 1.5 copy.47
  1863.8 1.3 copy.91
  1865.3 1.5 copy.46
  1866.8 1.1 reshape.43
  1868.9 4.8 reduce-scatter.25.cloned.1.call-done
  1873.7 1.2 copy.99
  1875.0 1.1 pad_maximum_fusion.8
  1876.1 397.7 %all-reduce.11.cloned.1.call-done = f32[16,512,768]{2,1,0:T(8,128)} async-done(((f32[16,512,768]{2,1,0:T(8,128)}), f32[16,512,768]{2,1,0:T(8,128)}) %all-reduce.11.cloned.1.call-update) | async-done | bytes 25165840 | tf_op jit(solution)/shard_map/psum | solution.py:40
  2273.8 17.5 add_convert_fusion
  (72 shorter events, 4.1 us)
Async XLA Ops:
  8.0 18.0 copy-start.9
  8.0 487.4 %all-reduce.5.cloned.1.call-start = ((), (), s32[]{:S(2)}) async-start(), calls=%async_computation.8 | async-start | bytes 50331648 | tf_op jit(solution)/shard_map/psum | solution.py:20
  26.0 28.7 %copy-start.11 = (bf16[2,768,768]{2,1,0:T(8,128)(2,1)S(1)}, bf16[2,768,768]{2,1,0:T(8,128)(2,1)}, u32[]{:S(2)}) copy-start(bf16[2,768,768]{2,1,0:T(8,128)(2,1)} %param.12) | copy-start | bytes 7077892
  73.4 1.5 copy-start.14
  73.5 1053.6 %all-reduce.7.cloned.1.call-start = ((), (), s32[]{:S(2)}) async-start(), calls=%async_computation.9 | async-start | bytes 50331648 | tf_op jit(solution)/shard_map/psum | solution.py:40
  495.4 17.3 copy-start.15
  508.2 4.4 copy-start.2
  517.1 31.4 %copy-start.5 = (bf16[16,512,3,64]{1,3,2,0:T(8,128)(2,1)}, bf16[16,512,3,64]{1,3,2,0:T(8,128)(2,1)S(1)}, u32[]{:S(2)}) copy-start(bf16[16,512,3,64]{1,3,2,0:T(8,128)(2,1)S(1)} %fusion.116) | copy-start | bytes 9437188
  612.3 64.1 %copy-start.6 = (bf16[16,512,3,64]{1,3,2,0:T(8,128)(2,1)S(1)}, bf16[16,512,3,64]{1,3,2,0:T(8,128)(2,1)}, u32[]{:S(2)}) copy-start(bf16[16,512,3,64]{1,3,2,0:T(8,128)(2,1)} %copy-done.5) | copy-start | bytes 9437188
  707.7 1.7 copy-start.12
  707.8 901.3 %all-reduce.9.cloned.1.call-start = ((), (), s32[]{:S(2)}) async-start(), calls=%async_computation.10 | async-start | bytes 50331648 | tf_op jit(solution)/shard_map/psum | solution.py:20
  727.9 416.5 %copy-start.10 = (bf16[2,768,768]{2,1,0:T(8,128)(2,1)S(1)}, bf16[2,768,768]{2,1,0:T(8,128)(2,1)}, u32[]{:S(2)}) copy-start(bf16[2,768,768]{2,1,0:T(8,128)(2,1)} %param.13) | copy-start | bytes 7077892
  1139.9 4.5 copy-start.1
  1144.4 26.9 %copy-start.13 = (bf16[2,768,768]{2,1,0:T(8,128)(2,1)S(1)}, bf16[2,768,768]{2,1,0:T(8,128)(2,1)}, u32[]{:S(2)}) copy-start(bf16[2,768,768]{2,1,0:T(8,128)(2,1)} %param.12) | copy-start | bytes 7077892
  1189.7 664.8 %reduce-scatter.39.cloned.1.call-start = ((), (), s32[]{:S(2)}) async-start(), calls=%async_computation.19 | async-start | bytes 2949120
  1209.0 646.9 %reduce-scatter.35.cloned.1.call-start = ((), (), s32[]{:S(2)}) async-start(), calls=%async_computation.17 | async-start | bytes 2949120
  1226.0 631.4 %reduce-scatter.31.cloned.1.call-start = ((), (), s32[]{:S(2)}) async-start(), calls=%async_computation.15 | async-start | bytes 983040
  1257.7 601.0 %reduce-scatter.27.cloned.1.call-start = ((), (), s32[]{:S(2)}) async-start(), calls=%async_computation.13 | async-start | bytes 2457600
  1274.8 586.1 %reduce-scatter.37.cloned.1.call-start = ((), (), s32[]{:S(2)}) async-start(), calls=%async_computation.18 | async-start | bytes 2949120
  1318.7 545.2 %reduce-scatter.33.cloned.1.call-start = ((), (), s32[]{:S(2)}) async-start(), calls=%async_computation.16 | async-start | bytes 2949120
  1363.1 503.7 %reduce-scatter.29.cloned.1.call-start = ((), (), s32[]{:S(2)}) async-start(), calls=%async_computation.14 | async-start | bytes 983040
  1622.0 4.8 copy-start
  1632.1 23.1 %copy-start.3 = (bf16[16,512,3,64]{1,3,2,0:T(8,128)(2,1)}, bf16[16,512,3,64]{1,3,2,0:T(8,128)(2,1)S(1)}, u32[]{:S(2)}) copy-start(bf16[16,512,3,64]{1,3,2,0:T(8,128)(2,1)S(1)} %fusion.119) | copy-start | bytes 9437188
  1740.3 64.2 %copy-start.4 = (bf16[16,512,3,64]{1,3,2,0:T(8,128)(2,1)S(1)}, bf16[16,512,3,64]{1,3,2,0:T(8,128)(2,1)}, u32[]{:S(2)}) copy-start(bf16[16,512,3,64]{1,3,2,0:T(8,128)(2,1)} %copy-done.3) | copy-start | bytes 9437188
  1818.0 19.1 copy-start.7
  1818.1 55.6 %reduce-scatter.25.cloned.1.call-start = ((), (), s32[]{:S(2)}) async-start(), calls=%async_computation.12 | async-start | bytes 2457600
  1837.1 436.7 %all-reduce.11.cloned.1.call-start = ((), (), s32[]{:S(2)}) async-start(), calls=%async_computation.11 | async-start | bytes 50331648 | tf_op jit(solution)/shard_map/psum | solution.py:40
  1862.3 12.6 copy-start.8
Sparse Core Ops, SparseCore 0:
  73.6 421.7 all-reduce.4
  707.9 419.1 all-reduce.6
  1189.8 419.1 all-reduce.8
  1854.6 419.1 all-reduce.10
Sparse Core Ops, SparseCore 1:
  1209.1 33.5 reduce-scatter.38
  1245.5 33.3 reduce-scatter.34
  1282.2 22.3 reduce-scatter.30
  1307.6 30.0 reduce-scatter.26
  1340.7 33.3 reduce-scatter.36
  1377.1 33.3 reduce-scatter.32
  1818.1 22.5 reduce-scatter.28
  1843.6 30.0 reduce-scatter.24
where the time goes:
time: 2310 us; the launch traced here: 2300 us
  waiting for transfers between devices  1400 us (61%)
  matrix products  720 us (31%)
  other arithmetic  114 us (5%)
  local copies, waits for them, and re-layouts  46.5 us (2%)
    psum x2, waiting for transfers between devices, layer_backward(): lax.psum(attn_part, 'tp')  797 us
    psum x2, waiting for transfers between devices, layer_backward(): lax.psum(mlp_part, 'tp')  600 us
    dot_general x2, matrix products, layer_backward(): jnp.einsum('bhqk,bqhe->bkhe', d_scores, q_heads, preferred_element_type=j...  128 us
    dot_general x2, matrix products, layer_backward(): jnp.einsum('bhqk,bkhe->bqhe', d_scores, k_heads, preferred_element_type=j...  128 us
    dot_general x2, matrix products, layer_backward(): jnp.einsum('bsd,fd->bsf', d_out, w_down, preferred_element_type=jnp.float32)  55.6 us
    convert_element_type x2, other arithmetic, layer_backward(): prob_bf = attn_prob.astype(jnp.bfloat16)  54.8 us
    dot_general x2, matrix products, layer_backward(): jnp.einsum('bqhe,bkhe->bhqk', d_ctx, v_heads, preferred_element_type=jnp....  52.7 us
    sub x2, matrix products, layer_backward(): attn_prob = jax.nn.softmax(scores, axis=-1)  50 us
  transfers between devices with their start and end apart: 12, of which 5 were waited for; matrix products, arithmetic and copies ran while one was open for 22% of the time, Pallas kernels for 0%

commit v1 on v0

v1 whole, which is shorter than its diff:
```python
import jax
import jax.numpy as jnp
from jax import lax
from jax.sharding import PartitionSpec as P

DATA_AXES = ('dpy', 'dpx')
ALL_AXES = ('dpy', 'dpx', 'tp')
F32 = jnp.float32
BF16 = jnp.bfloat16


def layer_backward(x_in, y_mid, d_out, w_qkv, w_out, w_up, w_down):
    head_dim = w_qkv.shape[-1]
    attn_scale = head_dim ** -0.5
    h_pre = jnp.einsum('bsd,df->bsf', y_mid, w_up, preferred_element_type=F32)
    gelu_out, gelu_pull = jax.vjp(jax.nn.gelu, h_pre)
    gelu_bf = gelu_out.astype(BF16)
    g_down = jnp.einsum('bsf,bsd->fd', gelu_bf, d_out, preferred_element_type=F32)
    d_gelu = jnp.einsum('bsd,fd->bsf', d_out, w_down, preferred_element_type=F32)
    d_pre = gelu_pull(d_gelu)[0].astype(BF16)
    g_up = jnp.einsum('bsd,bsf->df', y_mid, d_pre, preferred_element_type=F32)
    mlp = jnp.einsum('bsf,df->bsd', d_pre, w_up, preferred_element_type=F32)
    d_mid = (d_out.astype(F32) + mlp).astype(BF16)
    qkv_act = jnp.einsum('bsd,dche->bsche', x_in, w_qkv, preferred_element_type=F32).astype(BF16)
    q_heads = qkv_act[:, :, 0]
    k_heads = qkv_act[:, :, 1]
    v_heads = qkv_act[:, :, 2]
    scores = jnp.einsum('bqhe,bkhe->bhqk', q_heads, k_heads, preferred_element_type=F32) * attn_scale
    attn_prob = jax.nn.softmax(scores, axis=-1)
    prob_bf = attn_prob.astype(BF16)
    context = jnp.einsum('bhqk,bkhe->bqhe', prob_bf, v_heads, preferred_element_type=F32).astype(BF16)
    g_out = jnp.einsum('crif,cre->ife', context, d_mid, preferred_element_type=F32)
    d_ctx = jnp.einsum('cre,ife->crif', d_mid, w_out, preferred_element_type=F32).astype(BF16)
    d_prob = jnp.einsum('bqhe,bkhe->bhqk', d_ctx, v_heads, preferred_element_type=F32)
    d_val = jnp.einsum('bhqk,bqhe->bkhe', prob_bf, d_ctx, preferred_element_type=F32).astype(BF16)
    row_dot = jnp.sum(d_prob * attn_prob, axis=-1, keepdims=True)
    d_scores = (attn_prob * (d_prob - row_dot) * attn_scale).astype(BF16)
    d_query = jnp.einsum('bhqk,bkhe->bqhe', d_scores, k_heads, preferred_element_type=F32).astype(BF16)
    d_key = jnp.einsum('bhqk,bqhe->bkhe', d_scores, q_heads, preferred_element_type=F32).astype(BF16)
    d_qkv = jnp.stack([d_query, d_key, d_val], axis=2)
    g_qkv = jnp.einsum('bsd,bsche->dche', x_in, d_qkv, preferred_element_type=F32)
    attn = jnp.einsum('bsche,dche->bsd', d_qkv, w_qkv, preferred_element_type=F32)
    d_input = (d_mid.astype(F32) + attn).astype(BF16)
    return d_input, (g_qkv, g_out, g_up, g_down)


def solution(mesh):
    dp = mesh.shape['dpy'] * mesh.shape['dpx']
    tp = mesh.shape['tp']
    act_spec = P(None, DATA_AXES, None, None)

    def reduce_grads(grads):
        g_qkv, g_out, g_up, g_down = grads
        d = g_up.shape[0]
        f = g_up.shape[1]
        nh, hd = g_out.shape[0], g_out.shape[1]

        def rs(g):
            return lax.psum_scatter(g.reshape((dp * tp,) + g.shape[2:]), ALL_AXES, scatter_dimension=0, tiled=True)[0] / dp
        a = rs(g_qkv.reshape(dp, d // dp, 3, tp, nh // tp, hd).transpose(0, 3, 1, 2, 4, 5).reshape(dp, tp, d // dp, -1))
        a = a.reshape(d // dp, 3, nh // tp, hd)
        b = rs(g_out.reshape(tp, nh // tp * hd, dp, d // dp).transpose(2, 0, 1, 3))
        b = b.reshape(nh // tp, hd, d // dp)
        c = rs(g_up.reshape(dp, d // dp, tp, f // tp).transpose(0, 2, 1, 3))
        e = rs(g_down.reshape(tp, dp, f // tp // dp, d).transpose(1, 0, 2, 3))
        return a, b, c, e

    def device_backward(x_saved, y_saved, dz_top, w_qkv, w_out, w_up, w_down):
        t = lax.axis_index('tp')
        nb = dz_top.shape[0] // tp
        layers = range(x_saved.shape[0])
        w_up, w_down, w_qkv, w_out = [list(w) for w in (w_up, w_down, w_qkv, w_out)]
        for l in reversed(layers):
            w_up[l] = lax.all_gather(w_up[l], 'tp', axis=1, tiled=True)
            w_down[l] = lax.all_gather(w_down[l], 'tp', axis=0, tiled=True)
            w_qkv[l] = lax.all_gather(w_qkv[l], 'tp', axis=2, tiled=True)
            w_out[l] = lax.all_gather(w_out[l], 'tp', axis=0, tiled=True)
        x = lax.dynamic_slice_in_dim(x_saved, t * nb, nb, axis=1)
        y = lax.dynamic_slice_in_dim(y_saved, t * nb, nb, axis=1)
        grad_in = lax.dynamic_slice_in_dim(dz_top, t * nb, nb, axis=0)
        reduced = []
        for l in reversed(layers):
            grad_in, grads = layer_backward(x[l], y[l], grad_in, w_qkv[l], w_out[l], w_up[l], w_down[l])
            reduced.insert(0, reduce_grads(grads))
        stacked = tuple(jnp.stack([g[i] for g in reduced]) for i in range(4))
        grad_in = lax.all_gather(grad_in, 'tp', axis=0, tiled=True)
        return (grad_in,) + stacked

    return jax.shard_map(device_backward, mesh=mesh,
                         in_specs=(act_spec, act_spec, P(DATA_AXES, None, None), P(None, None, None, 'tp', None), P(None, 'tp', None, None), P(None, None, 'tp'), P(None, 'tp', None)),
                         out_specs=(P(DATA_AXES, None, None), P(None, DATA_AXES, None, 'tp', None), P(None, 'tp', None, DATA_AXES), P(None, DATA_AXES, 'tp'), P(None, ('tp', 'dpy', 'dpx'), None)),
                         check_vma=False)
```

time: 2310 us -> 1370 us (0.59)
  waiting for transfers between devices: 1400 us -> 368 us
  local copies, waits for them, and re-layouts: 46.5 us -> 163 us
  other arithmetic: 114 us -> 82.9 us
    psum x4 -> x0, waiting for transfers between devices: 1400 us -> none  [the longest x2 797 us: layer_backward(): lax.psum(attn_part, 'tp')]
    reduce_scatter x0 -> x8, waiting for transfers between devices: none -> 270 us  [rs(): lax.psum_scatter(g.reshape((dp * tp,) + g.shape[2:]), ALL_AXES, scatter_d...]
    dot_general x0 -> x10, local copies, waits for them, and re-layouts: none -> 110 us  [the longest x7 99.5 us: layer_backward(): g_up = jnp.einsum('bsd,bsf->df', y_mid, d_pre, preferred_element_type=F32)]
    all_gather x0 -> x9, waiting for transfers between devices: none -> 95.9 us  [the longest x1 80.7 us: device_backward(): grad_in = lax.all_gather(grad_in, 'tp', axis=0, tiled=True)]
    convert_element_type x6 -> x2, other arithmetic: 111 us -> 54.8 us  [layer_backward(): prob_bf = attn_prob.astype(BF16)]
    unnamed x52 -> x34, local copies, waits for them, and re-layouts: 46.5 us -> 15 us
  transfers between devices with their start and end apart: 12 -> 17, of which waited for: 5 -> 6; matrix products, arithmetic and copies ran while one was open for 22% -> 70% of each run, Pallas kernels for 0% -> 0%
where the time goes in v1:
time: 1370 us; the launch traced here: 1350 us
  matrix products  725 us (53%)
  waiting for transfers between devices  368 us (27%)
  local copies, waits for them, and re-layouts  163 us (12%)
  other arithmetic  82.9 us (6%)
  between operations  14.7 us (1%)
    reduce_scatter x8, waiting for transfers between devices, rs(): lax.psum_scatter(g.reshape((dp * tp,) + g.shape[2:]), ALL_AXES, scatter_d...  270 us
    dot_general x2, matrix products, layer_backward(): jnp.einsum('bhqk,bqhe->bkhe', d_scores, q_heads, preferred_element_type=F32)  128 us
    dot_general x2, matrix products, layer_backward(): jnp.einsum('bhqk,bkhe->bqhe', d_scores, k_heads, preferred_element_type=F32)  128 us
    dot_general x7, local copies, waits for them, and re-layouts, layer_backward(): g_up = jnp.einsum('bsd,bsf->df', y_mid, d_pre, preferred_element_type=F32)  99.5 us
    all_gather x1, waiting for transfers between devices, device_backward(): grad_in = lax.all_gather(grad_in, 'tp', axis=0, tiled=True)  80.7 us
    dot_general x2, matrix products, layer_backward(): h_pre = jnp.einsum('bsd,df->bsf', y_mid, w_up, preferred_element_type=F32)  68.6 us
    dot_general x2, matrix products, layer_backward(): mlp = jnp.einsum('bsf,df->bsd', d_pre, w_up, preferred_element_type=F32)  61.4 us
    convert_element_type x2, other arithmetic, layer_backward(): prob_bf = attn_prob.astype(BF16)  54.8 us
  transfers between devices with their start and end apart: 17, of which 6 were waited for; matrix products, arithmetic and copies ran while one was open for 70% of the time, Pallas kernels for 0%

profile of v1, /device:TPU:0, one launch (start us, length us, event | category | flops | bytes accessed | tf_op | source)
XLA Modules:
  0.0 1354.5 jit_solution(16733098471422103427)
XLA Ops:
  7.2 3.0 fusion.246
  11.1 3.2 fusion.244
  14.3 1.6 fusion.245
  19.0 4.9 dynamic-slice_bitcast_fusion
  23.9 2.8 copy.68
  26.7 15.2 %all-gather.24.cloned.1.call-done = bf16[1,768,3,12,64]{1,4,3,2,0:T(8,128)(2,1)} async-done(((bf16[1,768,3,3,64]{1,4,3,2,0:T(8,128)(2,1)}), bf16[1,768,3,12,64]{1,4,3,2,0:T(8,128)(2,1)}) %all-gather.24.cloned.1.call-update) | async-done | bytes 3538960 | tf_op jit(solution)/shard_map/all_gather | solution.py:76
  41.9 12.4 convolution_convert_fusion.1
  54.3 24.7 %fusion.247 = (f32[4,12,512]{2,1,0:T(8,128)S(1)}, f32[4,12,512,512]{2,3,1,0:T(8,128)}) fusion(bf16[4,512,3,12,64]{1,4,3,2,0:T(8,128)(2,1)} %convolution_convert_fusion.1), kind=kOutput, calls=%fused_computation.229 | convolution fusion | flops 1648361984 | bytes 56721408 | tf_op jit(solution)/shard_map/sub | solution.py:29
  78.9 12.5 convolution_convert_fusion
  91.5 25.0 %fusion.248 = (f32[4,12,512]{2,1,0:T(8,128)S(1)}, f32[4,12,512,512]{2,3,1,0:T(8,128)}) fusion(bf16[4,512,3,12,64]{1,4,3,2,0:T(8,128)(2,1)} %convolution_convert_fusion), kind=kOutput, calls=%fused_computation.230 | convolution fusion | flops 1648361984 | bytes 56721408 | tf_op jit(solution)/shard_map/sub | solution.py:29
  116.4 27.4 %fusion.242 = bf16[4,12,512,512]{2,3,1,0:T(8,128)(2,1)} fusion(f32[4,12,512,512]{2,3,1,0:T(8,128)} %get-tuple-element.18, f32[4,12,512]{2,1,0:T(8,128)S(1)} %get-tuple-element.17), kind=kLoop, calls=%fused_computation.224 | loop fusion | flops 25165824 | bytes 75595776 | tf_op jit(solution)/shard_map/convert_element_type | solution.py:30
  143.9 27.3 %fusion.243 = bf16[4,12,512,512]{2,3,1,0:T(8,128)(2,1)} fusion(f32[4,12,512,512]{2,3,1,0:T(8,128)} %get-tuple-element.20, f32[4,12,512]{2,1,0:T(8,128)S(1)} %get-tuple-element.19), kind=kLoop, calls=%fused_computation.225 | loop fusion | flops 25165824 | bytes 75595776 | tf_op jit(solution)/shard_map/convert_element_type | solution.py:30
  171.2 17.5 %fusion.98 = f32[4,512,3072]{2,1,0:T(8,128)} fusion(bf16[1,3072,768]{2,1,0:T(8,128)(2,1)} %all-gather.20.cloned.1.call-done, bf16[16,512,768]{2,1,0:T(8,128)(2,1)} %param.9, s32[]{:T(128)S(6)} %select_n.2), kind=kOutput, calls=%fused_computation.110 | convolution fusion | flops 9663676416 | bytes 33030148 | tf_op jit(solution)/shard_map/bsd,fd->bsf/dot_general | solution.py:19
  188.7 34.6 %fusion.39 = (bf16[3072,4,512]{0,2,1:T(8,128)(2,1)}, f32[4,512,3072]{2,1,0:T(8,128)}) fusion(f32[4,512,3072]{2,1,0:T(8,128)} %fusion.98, bf16[1,768,3072]{2,1,0:T(8,128)(2,1)} %all-gather.22.cloned.1.call-done, bf16[2,16,512,768]{3,2,1,0:T(8,128)(2,1)} %param.8, s32[]{:T(128)S(6)} %add.72, s32[]{:T(128)S(6)} %select_n.2), kind=kOutput, calls=%fused_computation.51 | convolution fusion | flops 9789505536 | bytes 70778888 | tf_op jit(solution)/shard_map/bsd,df->bsf/dot_general | solution.py:15
  223.4 30.7 %add_convert_fusion.1 = bf16[4,512,768]{2,1,0:T(8,128)(2,1)} fusion(bf16[1,768,3072]{2,1,0:T(8,128)(2,1)S(1)} %copy-done.14, f32[4,512,3072]{2,1,0:T(8,128)} %get-tuple-element.22, f32[4,512,3072]{2,1,0:T(8,128)} %fusion.98, bf16[16,512,768]{2,1,0:T(8,128)(2,1)} %param.9, s32[]{:T(128)S(6)} %select_n.2), kind=kOutput, calls=%fused_computation.99 | convolution fusion | flops 9794224128 | bytes 61341700 | tf_op jit(solution)/shard_map/bsf,df->bsd/dot_general | solution.py:22
  254.1 4.8 fusion.166
  259.0 22.6 %fusion.240 = f32[4,12,512,512]{2,3,1,0:T(8,128)} fusion(bf16[4,512,12,64]{1,3,2,0:T(8,128)(2,1)S(1)} %fusion.166, bf16[4,512,3,12,64]{1,4,3,2,0:T(8,128)(2,1)} %convolution_convert_fusion.1), kind=kOutput, calls=%fused_computation.222 | convolution fusion | flops 1610612736 | bytes 56623104 | tf_op jit(solution)/shard_map/bqhe,bkhe->bhqk/dot_general | solution.py:34
  281.6 64.1 %convert_bitcast_fusion.5 = bf16[4,512,1,12,64]{1,4,3,0,2:T(8,128)(2,1)} fusion(f32[4,12,512,512]{2,3,1,0:T(8,128)} %fusion.240, bf16[4,512,3,12,64]{1,4,3,2,0:T(8,128)(2,1)} %convolution_convert_fusion.1, f32[4,12,512,512]{2,3,1,0:T(8,128)} %get-tuple-element.18, f32[4,12,512]{2,1,0:T(8,128)S(1)} %copy-done.13), kind=kOutput, calls=%fused_computation.153 | convolution fusion | flops 1700291072 | bytes 207880192 | tf_op jit(solution)/shard_map/bhqk,bkhe->bqhe/dot_general | solution.py:38
  345.7 64.0 %convert_bitcast_fusion.4 = bf16[4,512,1,12,64]{1,4,3,0,2:T(8,128)(2,1)} fusion(f32[4,12,512,512]{2,3,1,0:T(8,128)} %fusion.240, bf16[4,512,3,12,64]{1,4,3,2,0:T(8,128)(2,1)} %convolution_convert_fusion.1, f32[4,12,512,512]{2,3,1,0:T(8,128)} %get-tuple-element.18, f32[4,12,512]{2,1,0:T(8,128)S(1)} %copy-done.13), kind=kOutput, calls=%fused_computation.152 | convolution fusion | flops 1700291072 | bytes 207880192 | tf_op jit(solution)/shard_map/bhqk,bqhe->bkhe/dot_general | solution.py:39
  409.7 13.0 convert_bitcast_fusion.3
  422.7 13.8 %fusion.89 = bf16[4,512,768]{2,1,0:T(8,128)(2,1)} fusion(bf16[4,512,768]{2,1,0:T(8,128)(2,1)} %add_convert_fusion.1, bf16[1,768,3,12,64]{1,4,3,2,0:T(8,128)(2,1)} %all-gather.24.cloned.1.call-done, bf16[4,512,1,12,64]{1,4,3,0,2:T(8,128)(2,1)S(1)} %convert_bitcast_fusion.3, bf16[4,512,1,12,64]{1,4,3,0,2:T(8,128)(2,1)} %convert_bitcast_fusion.4, ...), kind=kOutput, calls=%fused_computation.97 | convolution fusion | flops 7261913088 | bytes 19267584 | tf_op jit(solution)/shard_map/bsche,dche->bsd/dot_general | solution.py:42
  436.5 18.0 %fusion.93 = f32[4,512,3072]{2,1,0:T(8,128)} fusion(bf16[4,512,768]{2,1,0:T(8,128)(2,1)} %fusion.89, bf16[1,3072,768]{2,1,0:T(8,128)(2,1)} %all-gather.28.cloned.1.call-done), kind=kOutput, calls=%fused_computation.105 | convolution fusion | flops 9663676416 | bytes 33030144 | tf_op jit(solution)/shard_map/bsd,fd->bsf/dot_general | solution.py:19
  454.5 34.0 %fusion.32 = (bf16[3072,4,512]{0,2,1:T(8,128)(2,1)}, f32[4,512,3072]{2,1,0:T(8,128)}) fusion(f32[4,512,3072]{2,1,0:T(8,128)} %fusion.93, bf16[1,768,3072]{2,1,0:T(8,128)(2,1)} %all-gather.30.cloned.1.call-done, bf16[2,16,512,768]{3,2,1,0:T(8,128)(2,1)} %param.8, s32[]{:T(128)S(6)} %select_n.2), kind=kOutput, calls=%fused_computation.44 | convolution fusion | flops 9789505536 | bytes 70778880 | tf_op jit(solution)/shard_map/bsd,df->bsf/dot_general | solution.py:15
  488.5 30.7 %add_convert_fusion = bf16[4,512,768]{2,1,0:T(8,128)(2,1)} fusion(bf16[4,512,768]{2,1,0:T(8,128)(2,1)} %fusion.89, bf16[1,768,3072]{2,1,0:T(8,128)(2,1)S(1)} %copy-done.15, f32[4,512,3072]{2,1,0:T(8,128)} %get-tuple-element.24, f32[4,512,3072]{2,1,0:T(8,128)} %fusion.93), kind=kOutput, calls=%fused_computation.98 | convolution fusion | flops 9794224128 | bytes 61341696 | tf_op jit(solution)/shard_map/bsf,df->bsd/dot_general | solution.py:22
  519.2 14.4 %fusion.184 = f32[12,64,768]{2,1,0:T(8,128)} fusion(bf16[4,512,768]{2,1,0:T(8,128)(2,1)} %add_convert_fusion, bf16[4,12,512,512]{2,3,1,0:T(8,128)(2,1)} %fusion.243, bf16[4,512,3,12,64]{1,4,3,2,0:T(8,128)(2,1)} %convolution_convert_fusion), kind=kOutput, calls=%fused_computation.168 | convolution fusion | flops 4028104704 | bytes 33816576 | tf_op jit(solution)/shard_map/crif,cre->ife/dot_general | solution.py:32
  533.5 3.6 reshape.106
  537.2 2.2 copy.78
  539.4 14.6 %fusion.193 = f32[12,64,768]{2,1,0:T(8,128)} fusion(bf16[4,512,768]{2,1,0:T(8,128)(2,1)} %add_convert_fusion.1, bf16[4,12,512,512]{2,3,1,0:T(8,128)(2,1)} %fusion.242, bf16[4,512,3,12,64]{1,4,3,2,0:T(8,128)(2,1)} %convolution_convert_fusion.1), kind=kOutput, calls=%fused_computation.169 | convolution fusion | flops 4028104704 | bytes 33816576 | tf_op jit(solution)/shard_map/crif,cre->ife/dot_general | solution.py:32
  554.0 3.6 reshape.108
  557.6 2.2 copy.81
  560.0 4.8 fusion.169
  564.8 22.5 %fusion.241 = f32[4,12,512,512]{2,3,1,0:T(8,128)} fusion(bf16[4,512,12,64]{1,3,2,0:T(8,128)(2,1)S(1)} %fusion.169, bf16[4,512,3,12,64]{1,4,3,2,0:T(8,128)(2,1)} %convolution_convert_fusion), kind=kOutput, calls=%fused_computation.223 | convolution fusion | flops 1610612736 | bytes 56623104 | tf_op jit(solution)/shard_map/bqhe,bkhe->bhqk/dot_general | solution.py:34
  587.3 63.9 %convert_bitcast_fusion.2 = bf16[4,512,1,12,64]{1,4,3,0,2:T(8,128)(2,1)} fusion(f32[4,12,512,512]{2,3,1,0:T(8,128)} %fusion.241, bf16[4,512,3,12,64]{1,4,3,2,0:T(8,128)(2,1)} %convolution_convert_fusion, f32[4,12,512,512]{2,3,1,0:T(8,128)} %get-tuple-element.20, f32[4,12,512]{2,1,0:T(8,128)S(1)} %copy-done.11), kind=kOutput, calls=%fused_computation.150 | convolution fusion | flops 1700291072 | bytes 207880192 | tf_op jit(solution)/shard_map/bhqk,bkhe->bqhe/dot_general | solution.py:38
  651.2 13.0 convert_bitcast_fusion
  664.3 64.4 %convert_bitcast_fusion.1 = bf16[4,512,1,12,64]{1,4,3,0,2:T(8,128)(2,1)} fusion(f32[4,12,512,512]{2,3,1,0:T(8,128)} %fusion.241, bf16[4,512,3,12,64]{1,4,3,2,0:T(8,128)(2,1)} %convolution_convert_fusion, f32[4,12,512,512]{2,3,1,0:T(8,128)} %get-tuple-element.20, f32[4,12,512]{2,1,0:T(8,128)S(1)} %copy-done.11), kind=kOutput, calls=%fused_computation.149 | convolution fusion | flops 1700291072 | bytes 207880192 | tf_op jit(solution)/shard_map/bhqk,bqhe->bkhe/dot_general | solution.py:39
  728.6 6.9 pad_maximum_fusion.1
  735.6 14.1 %fusion.106 = f32[4,4,192,3,3,64]{2,5,4,1,3,0:T(8,128)S(1)} fusion(bf16[3,4,3,64,4,512]{5,3,2,1,4,0:T(8,128)(2,1)} %bitcast.388, bf16[4,192,4,512,1,1,1]{3,1,0,2,6,5,4:T(8,128)(2,1)} %bitcast.390), kind=kOutput, calls=%fused_computation.118 | convolution fusion | flops 7247757312 | bytes 19660800 | tf_op jit(solution)/shard_map/bsd,bsche->dche/dot_general | solution.py:41
  749.7 4.6 copy.71
  754.4 1.8 copy-done
  756.2 3.0 copy.72
  759.2 8.6 pad_maximum_fusion
  767.8 13.1 fusion.109
  780.9 4.8 copy.75
  785.8 17.1 %fusion.72 = f32[3072,768,1]{1,0,2:T(8,128)S(1)} fusion(bf16[4,512,768]{2,1,0:T(8,128)(2,1)} %fusion.89, f32[4,512,3072]{2,1,0:T(8,128)} %get-tuple-element.24), kind=kOutput, calls=%fused_computation.80 | convolution fusion | flops 9720299520 | bytes 37748736 | tf_op jit(solution)/shard_map/bsf,bsd->fd/dot_general | solution.py:18
  802.9 4.2 copy.89
  807.2 17.3 %fusion.73 = f32[3072,768,1]{1,0,2:T(8,128)S(1)} fusion(f32[4,512,3072]{2,1,0:T(8,128)} %get-tuple-element.22, bf16[16,512,768]{2,1,0:T(8,128)(2,1)} %param.9, s32[]{:T(128)S(6)} %select_n.2), kind=kOutput, calls=%fused_computation.81 | convolution fusion | flops 9720299520 | bytes 37748740 | tf_op jit(solution)/shard_map/bsf,bsd->fd/dot_general | solution.py:18
  824.5 4.2 copy.91
  828.7 4.9 dynamic-slice_bitcast_fusion.1
  833.7 4.7 copy.82
  838.4 23.5 %dot_general.172 = bf16[4,768,4,512]{1,0,3,2:T(4,128)(2,1)} reshape(bf16[3072,4,512]{0,2,1:T(8,128)(2,1)} %get-tuple-element.23) | data formatting | bytes 25165824 | tf_op jit(solution)/shard_map/bsd,bsf->df/dot_general | solution.py:21
  861.9 19.9 %copy.84 = bf16[4,768,4,512]{3,1,2,0:T(8,128)(2,1)} copy(bf16[4,768,4,512]{1,0,3,2:T(4,128)(2,1)} %dot_general.172) | data formatting | bytes 25165824 | tf_op jit(solution)/shard_map/bsd,bsf->df/dot_general | solution.py:21
  881.8 16.0 %fusion.70 = f32[4,192,4,768,1]{3,1,4,2,0:T(8,128)} fusion(bf16[4,768,4,512]{3,1,2,0:T(8,128)(2,1)} %copy.84, bf16[4,192,4,512,1]{3,1,0,2,4:T(8,128)(2,1)} %bitcast.391), kind=kOutput, calls=%fused_computation.78 | convolution fusion | flops 9663676416 | bytes 25165824 | tf_op jit(solution)/shard_map/bsd,bsf->df/dot_general | solution.py:21
  897.9 3.1 copy.85
  901.0 23.4 %dot_general.178 = bf16[4,768,4,512]{1,0,3,2:T(4,128)(2,1)} reshape(bf16[3072,4,512]{0,2,1:T(8,128)(2,1)} %get-tuple-element.21) | data formatting | bytes 25165824 | tf_op jit(solution)/shard_map/bsd,bsf->df/dot_general | solution.py:21
  924.4 19.9 %copy.87 = bf16[4,768,4,512]{3,1,2,0:T(8,128)(2,1)} copy(bf16[4,768,4,512]{1,0,3,2:T(4,128)(2,1)} %dot_general.178) | data formatting | bytes 25165824 | tf_op jit(solution)/shard_map/bsd,bsf->df/dot_general | solution.py:21
  944.4 15.1 %fusion.68 = f32[4,192,4,768,1]{3,1,4,2,0:T(8,128)} fusion(bf16[4,768,4,512]{3,1,2,0:T(8,128)(2,1)} %copy.87, bf16[4,192,4,512,1]{3,1,0,2,4:T(8,128)(2,1)S(1)} %bitcast.392), kind=kOutput, calls=%fused_computation.76 | convolution fusion | flops 9663676416 | bytes 25165824 | tf_op jit(solution)/shard_map/bsd,bsf->df/dot_general | solution.py:21
  959.5 1.8 copy-done.2
  961.3 12.7 fusion.88
  980.1 22.0 %reduce-scatter.21.cloned.1.call-done = f32[1,192,768]{2,1,0:T(8,128)} async-done(((f32[16,192,768]{2,1,0:T(8,128)}), f32[1,192,768]{2,1,0:T(8,128)}) %reduce-scatter.21.cloned.1.call-update) | async-done | bytes 589840 | tf_op jit(solution)/shard_map/reduce_scatter | solution.py:59
  1003.2 82.9 %reduce-scatter.23.cloned.1.call-done = f32[1,192,768]{2,1,0:T(8,128)} async-done(((f32[16,192,768]{2,1,0:T(8,128)}), f32[1,192,768]{2,1,0:T(8,128)}) %reduce-scatter.23.cloned.1.call-update) | async-done | bytes 589840 | tf_op jit(solution)/shard_map/reduce_scatter | solution.py:59
  1088.4 81.8 %reduce-scatter.17.cloned.1.call-done = f32[1,192,768]{2,1,0:T(8,128)} async-done(((f32[16,192,768]{2,1,0:T(8,128)}), f32[1,192,768]{2,1,0:T(8,128)}) %reduce-scatter.17.cloned.1.call-update) | async-done | bytes 589840 | tf_op jit(solution)/shard_map/reduce_scatter | solution.py:59
  1171.3 82.9 %reduce-scatter.19.cloned.1.call-done = f32[1,192,768]{2,1,0:T(8,128)} async-done(((f32[16,192,768]{2,1,0:T(8,128)}), f32[1,192,768]{2,1,0:T(8,128)}) %reduce-scatter.19.cloned.1.call-update) | async-done | bytes 589840 | tf_op jit(solution)/shard_map/reduce_scatter | solution.py:59
  1256.4 80.7 %all-gather.18.cloned.1.call-done = bf16[16,512,768]{2,1,0:T(8,128)(2,1)} async-done(((bf16[4,512,768]{2,1,0:T(8,128)(2,1)}), bf16[16,512,768]{2,1,0:T(8,128)(2,1)}) %all-gather.18.cloned.1.call-update) | async-done | bytes 12582928 | tf_op jit(solution)/shard_map/all_gather | solution.py:86
  1337.1 10.4 copy.185
  (88 shorter events, 17.1 us)
Async XLA Ops:
  7.2 7.1 copy-start.8
  7.2 8.8 copy-start.9
  7.2 34.7 %all-gather.24.cloned.1.call-start = ((), (), s32[]{:S(2)}) async-start(), calls=%async_computation.19 | async-start | bytes 4423680 | tf_op jit(solution)/shard_map/all_gather | solution.py:76
  10.3 68.7 %all-gather.32.cloned.1.call-start = ((), (), s32[]{:S(2)}) async-start(), calls=%async_computation.23 | async-start | bytes 4423680 | tf_op jit(solution)/shard_map/all_gather | solution.py:76
  11.0 160.2 %all-gather.20.cloned.1.call-start = ((), (), s32[]{:S(2)}) async-start(), calls=%async_computation.17 | async-start | bytes 5898240 | tf_op jit(solution)/shard_map/all_gather | solution.py:75
  14.3 174.5 %all-gather.22.cloned.1.call-start = ((), (), s32[]{:S(2)}) async-start(), calls=%async_computation.18 | async-start | bytes 5898240 | tf_op jit(solution)/shard_map/all_gather | solution.py:74
  15.9 238.2 %all-gather.26.cloned.1.call-start = ((), (), s32[]{:S(2)}) async-start(), calls=%async_computation.20 | async-start | bytes 1474560 | tf_op jit(solution)/shard_map/all_gather | solution.py:77
  16.8 419.7 %all-gather.28.cloned.1.call-start = ((), (), s32[]{:S(2)}) async-start(), calls=%async_computation.21 | async-start | bytes 5898240 | tf_op jit(solution)/shard_map/all_gather | solution.py:75
  17.4 437.1 %all-gather.30.cloned.1.call-start = ((), (), s32[]{:S(2)}) async-start(), calls=%async_computation.22 | async-start | bytes 5898240 | tf_op jit(solution)/shard_map/all_gather | solution.py:74
  18.2 541.8 %all-gather.34.cloned.1.call-start = ((), (), s32[]{:S(2)}) async-start(), calls=%async_computation.24 | async-start | bytes 1474560 | tf_op jit(solution)/shard_map/all_gather | solution.py:77
  18.9 955.2 %reduce-scatter.13.cloned.1.call-start = ((), (), s32[]{:S(2)}) async-start(), calls=%async_computation.11 | async-start | bytes 3342336 | tf_op jit(solution)/shard_map/reduce_scatter | solution.py:59
  78.9 37.5 %copy-start.12 = (f32[4,12,512]{2,1,0:T(8,128)}, f32[4,12,512]{2,1,0:T(8,128)S(1)}, u32[]{:S(2)}) copy-start(f32[4,12,512]{2,1,0:T(8,128)S(1)} %get-tuple-element.17) | copy-start | bytes 294916
  116.4 27.4 %copy-start.10 = (f32[4,12,512]{2,1,0:T(8,128)}, f32[4,12,512]{2,1,0:T(8,128)S(1)}, u32[]{:S(2)}) copy-start(f32[4,12,512]{2,1,0:T(8,128)S(1)} %get-tuple-element.19) | copy-start | bytes 294916
  188.7 34.7 %copy-start.14 = (bf16[1,768,3072]{2,1,0:T(8,128)(2,1)S(1)}, bf16[1,768,3072]{2,1,0:T(8,128)(2,1)}, u32[]{:S(2)}) copy-start(bf16[1,768,3072]{2,1,0:T(8,128)(2,1)} %all-gather.22.cloned.1.call-done) | copy-start | bytes 14155780
  258.9 22.7 %copy-start.4 = (bf16[4,512,12,64]{1,3,2,0:T(8,128)(2,1)}, bf16[4,512,12,64]{1,3,2,0:T(8,128)(2,1)S(1)}, u32[]{:S(2)}) copy-start(bf16[4,512,12,64]{1,3,2,0:T(8,128)(2,1)S(1)} %fusion.166) | copy-start | bytes 9437188
  259.0 22.6 %copy-start.13 = (f32[4,12,512]{2,1,0:T(8,128)S(1)}, f32[4,12,512]{2,1,0:T(8,128)}, u32[]{:S(2)}) copy-start(f32[4,12,512]{2,1,0:T(8,128)} %copy-done.12) | copy-start | bytes 294916
  422.7 13.8 %copy-start.3 = (bf16[4,512,1,12,64]{1,4,3,0,2:T(8,128)(2,1)}, bf16[4,512,1,12,64]{1,4,3,0,2:T(8,128)(2,1)S(1)}, u32[]{:S(2)}) copy-start(bf16[4,512,1,12,64]{1,4,3,0,2:T(8,128)(2,1)S(1)} %convert_bitcast_fusion.3) | copy-start | bytes 9437188
  454.5 34.0 %copy-start.15 = (bf16[1,768,3072]{2,1,0:T(8,128)(2,1)S(1)}, bf16[1,768,3072]{2,1,0:T(8,128)(2,1)}, u32[]{:S(2)}) copy-start(bf16[1,768,3072]{2,1,0:T(8,128)(2,1)} %all-gather.30.cloned.1.call-done) | copy-start | bytes 14155780
  559.9 415.2 %reduce-scatter.15.cloned.1.call-start = ((), (), s32[]{:S(2)}) async-start(), calls=%async_computation.12 | async-start | bytes 3342336 | tf_op jit(solution)/shard_map/reduce_scatter | solution.py:59
  564.8 22.5 %copy-start.5 = (bf16[4,512,12,64]{1,3,2,0:T(8,128)(2,1)}, bf16[4,512,12,64]{1,3,2,0:T(8,128)(2,1)S(1)}, u32[]{:S(2)}) copy-start(bf16[4,512,12,64]{1,3,2,0:T(8,128)(2,1)S(1)} %fusion.169) | copy-start | bytes 9437188
  564.8 22.5 %copy-start.11 = (f32[4,12,512]{2,1,0:T(8,128)S(1)}, f32[4,12,512]{2,1,0:T(8,128)}, u32[]{:S(2)}) copy-start(f32[4,12,512]{2,1,0:T(8,128)} %copy-done.10) | copy-start | bytes 294916
  664.2 64.5 %copy-start.1 = (bf16[4,512,1,12,64]{1,4,3,0,2:T(8,128)(2,1)}, bf16[4,512,1,12,64]{1,4,3,0,2:T(8,128)(2,1)S(1)}, u32[]{:S(2)}) copy-start(bf16[4,512,1,12,64]{1,4,3,0,2:T(8,128)(2,1)S(1)} %convert_bitcast_fusion) | copy-start | bytes 9437188
  664.2 312.6 %reduce-scatter.9.cloned.1.call-start = ((), (), s32[]{:S(2)}) async-start(), calls=%async_computation.9 | async-start | bytes 10027008 | tf_op jit(solution)/shard_map/reduce_scatter | solution.py:59
  754.3 1.9 copy-start
  754.3 223.6 %reduce-scatter.11.cloned.1.call-start = ((), (), s32[]{:S(2)}) async-start(), calls=%async_computation.10 | async-start | bytes 10027008 | tf_op jit(solution)/shard_map/reduce_scatter | solution.py:59
  759.2 8.6 copy-start.7
  785.7 216.4 %reduce-scatter.21.cloned.1.call-start = ((), (), s32[]{:S(2)}) async-start(), calls=%async_computation.15 | async-start | bytes 10027008 | tf_op jit(solution)/shard_map/reduce_scatter | solution.py:59
  807.1 279.0 %reduce-scatter.23.cloned.1.call-start = ((), (), s32[]{:S(2)}) async-start(), calls=%async_computation.16 | async-start | bytes 10027008 | tf_op jit(solution)/shard_map/reduce_scatter | solution.py:59
  828.7 341.5 %reduce-scatter.17.cloned.1.call-start = ((), (), s32[]{:S(2)}) async-start(), calls=%async_computation.13 | async-start | bytes 10027008 | tf_op jit(solution)/shard_map/reduce_scatter | solution.py:59
  897.8 356.4 %reduce-scatter.19.cloned.1.call-start = ((), (), s32[]{:S(2)}) async-start(), calls=%async_computation.14 | async-start | bytes 10027008 | tf_op jit(solution)/shard_map/reduce_scatter | solution.py:59
  924.4 19.9 %copy-start.6 = (bf16[768,4,512]{2,0,1:T(8,128)(2,1)S(1)}, bf16[768,4,512]{2,0,1:T(8,128)(2,1)}, u32[]{:S(2)}) copy-start(bf16[768,4,512]{2,0,1:T(8,128)(2,1)} %copy.85) | copy-start | bytes 9437188
  959.5 1.9 copy-start.2
  959.5 377.6 %all-gather.18.cloned.1.call-start = ((), (), s32[]{:S(2)}) async-start(), calls=%async_computation.8 | async-start | bytes 15728640 | tf_op jit(solution)/shard_map/all_gather | solution.py:86
Sparse Core Ops, SparseCore 0:
  10.4 31.4 all-gather.23
  43.4 28.6 all-gather.31
  74.2 35.4 all-gather.19
  111.6 35.4 all-gather.21
  148.5 15.3 all-gather.25
  165.8 35.4 all-gather.27
  203.4 35.4 all-gather.29
  241.0 15.3 all-gather.33
  560.0 54.4 reduce-scatter.12
  664.3 54.5 reduce-scatter.14
  754.4 79.4 reduce-scatter.8
  838.5 79.4 reduce-scatter.10
  922.7 79.4 reduce-scatter.20
  1006.7 79.4 reduce-scatter.22
  1090.7 79.4 reduce-scatter.16
  1174.8 79.4 reduce-scatter.18
  1256.2 80.8 all-gather.17

commit v2 on v0

v2 whole, which is shorter than its diff:
```python
import functools
import math

import jax
import jax.numpy as jnp
from jax import lax
from jax.experimental import pallas as pl
from jax.experimental.pallas import tpu as pltpu
from jax.sharding import PartitionSpec as P

DATA_AXES = ('dpy', 'dpx')
ALL_AXES = ('dpy', 'dpx', 'tp')
F32 = jnp.float32
BF16 = jnp.bfloat16
HEAD = 64
NN = (((1,), (0,)), ((), ()))
NT = (((1,), (1,)), ((), ()))
TN = (((0,), (0,)), ((), ()))
VMEM_LIMIT = 60 * 1024 * 1024


def dot(a, b, dims):
    return lax.dot_general(a, b, dims, preferred_element_type=F32)


def mlp_kernel(natural_dz, pos_ref, y_ref, dz_ref, w1_ref, w2_ref, dy_ref, g_ref, yt, dzt, acc, w1t, gt, dht):
    slot = pl.program_id(0)
    seqs, seq = y_ref.shape[-3], y_ref.shape[-2]
    dp, rows = g_ref.shape[0], g_ref.shape[3]

    @pl.when(slot == 0)
    def _():
        acc[...] = jnp.zeros_like(acc)
        for s in range(seqs):
            cols = slice(s * seq, (s + 1) * seq)
            yt[:, cols] = y_ref[0, s].T
            if natural_dz:
                dzt[:, cols] = dz_ref[s].T
    dz = dzt if natural_dz else dz_ref
    w1t[...] = w1_ref[0].T

    def block(i, carry):
        cols = pl.ds(pl.multiple_of(i * seq, seq), seq)
        h = dot(w1t[...], yt[:, cols], NN)
        dg = dot(w2_ref[0], dz[:, cols], NN)
        c0 = math.sqrt(2 / math.pi)
        c1 = 0.044715 * c0
        h2 = h * h
        t = jnp.tanh(h * (c0 + c1 * h2))
        q = 0.5 * t + 0.5
        g = h * q
        dh = dg * (q + (g * (1.0 - t)) * (c0 + (3 * c1) * h2))
        gt[:, cols] = g.astype(BF16)
        dh = dh.astype(BF16)
        dht[:, cols] = dh
        acc[:, cols] += dot(w1_ref[0], dh, NN)
        return carry
    lax.fori_loop(0, seqs, block, 0)
    g_down = dot(gt[...], dz[...], NT)
    for d in range(dp):
        g_ref[d, 0, 0] = g_down[d * rows:(d + 1) * rows]
    g_up = dot(yt[...], dht[...], NT)
    for d in range(dp):
        g_ref[d, 0, 1] = g_up[d * rows:(d + 1) * rows]

    @pl.when(slot == pl.num_programs(0) - 1)
    def _():
        dy_ref[...] = (dz[...].astype(F32) + acc[...]).astype(BF16)


def mlp_backward(pos, layer, y, dz, w1, w2, dp):
    slots, d, f = w1.shape
    natural = dz.ndim == 3
    seq = y.shape[2]
    seqs = y.shape[1] // slots
    tok = seqs * seq
    once = pl.Buffered(1)
    dz_spec = (pl.BlockSpec((seqs, seq, d), lambda j, p: (p[0], 0, 0), pipeline_mode=once) if natural
               else pl.BlockSpec((d, tok), lambda j, p: (0, 0), pipeline_mode=once))
    return pl.pallas_call(
        functools.partial(mlp_kernel, natural),
        out_shape=(jax.ShapeDtypeStruct((d, tok), BF16), jax.ShapeDtypeStruct((dp, slots, 2, d // dp, f), F32)),
        grid_spec=pltpu.PrefetchScalarGridSpec(
            num_scalar_prefetch=1, grid=(slots,),
            in_specs=[pl.BlockSpec((1, seqs, seq, d), lambda j, p: (layer, p[0], 0, 0), pipeline_mode=once), dz_spec,
                      pl.BlockSpec((1, d, f), lambda j, p: (j, 0, 0)), pl.BlockSpec((1, f, d), lambda j, p: (j, 0, 0))],
            out_specs=[pl.BlockSpec((d, tok), lambda j, p: (0, 0), pipeline_mode=once),
                       pl.BlockSpec((dp, 1, 2, d // dp, f), lambda j, p: (0, j, 0, 0, 0))],
            scratch_shapes=[pltpu.VMEM((d, tok), BF16), pltpu.VMEM((d, tok), BF16), pltpu.VMEM((d, tok), F32),
                            pltpu.VMEM((f, d), BF16), pltpu.VMEM((f, tok), BF16), pltpu.VMEM((f, tok), BF16)]),
        compiler_params=pltpu.CompilerParams(vmem_limit_bytes=VMEM_LIMIT, dimension_semantics=('arbitrary',)),
        cost_estimate=pl.CostEstimate(flops=10 * tok * d * f * slots, bytes_accessed=4 * d * f * 3 * slots, transcendentals=tok * f * slots),
        name='mlp_backward',
    )(pos, y, dz, w1, w2)


def attn_kernel(natural_out, pos_ref, x_ref, dy_ref, w_ref, dx_ref, g_ref, xt, acc, gacc, wt, qkv, do, b1, b2):
    slot, s = pl.program_id(0), pl.program_id(1)
    seq, d = x_ref.shape[-2:]
    dp, rows = g_ref.shape[0], g_ref.shape[2]
    nqkv = qkv.shape[0]
    third = nqkv // 3
    cols = pl.ds(pl.multiple_of(s * seq, seq), seq)

    @pl.when(slot == 0)
    def _():
        xt[:, cols] = x_ref[0, 0].T
        acc[:, cols] = jnp.zeros((d, seq), F32)

    @pl.when(s == 0)
    def _():
        wt[...] = w_ref[0].T
        gacc[...] = jnp.zeros_like(gacc)
        b1[pl.ds(nqkv, d - nqkv), :] = jnp.zeros((d - nqkv, seq), BF16)
        b2[pl.ds(0, b2.shape[0] - third), :] = jnp.zeros((b2.shape[0] - third, seq), BF16)
    x_t = xt[:, cols]
    dy_t = dy_ref[:, cols]
    qkv[...] = dot(w_ref[0, pl.ds(0, nqkv), :], x_t, NN).astype(BF16)
    do[...] = dot(w_ref[0, pl.ds(nqkv, d - nqkv), :], dy_t, NN).astype(BF16)
    scale = HEAD ** -0.5
    exp_scale = scale * math.log2(math.e)
    for h in range(third // HEAD):
        r = slice(h * HEAD, (h + 1) * HEAD)
        q_t = qkv[r, :]
        k_t = qkv[slice(third + h * HEAD, third + (h + 1) * HEAD), :]
        v_t = qkv[slice(2 * third + h * HEAD, 2 * third + (h + 1) * HEAD), :]
        do_t = do[r, :]
        do_s = do_t * scale
        k_n = k_t.T
        v_n = v_t.T
        dv = jnp.zeros((HEAD, seq), F32)
        dk = jnp.zeros((HEAD, seq), F32)
        qb = 256
        for c in range(seq // qb):
            qc = slice(c * qb, (c + 1) * qb)
            sc = dot(k_n, q_t[:, qc], NN)
            m = jnp.max(sc, axis=0, keepdims=True)
            e = jnp.exp2((sc - m) * exp_scale)
            p = e * (1.0 / jnp.sum(e, axis=0, keepdims=True))
            p_bf = p.astype(BF16)
            dp_t = dot(v_n, do_s[:, qc], NN)
            rd = jnp.sum(p * dp_t, axis=0, keepdims=True)
            ds = (p * (dp_t - rd)).astype(BF16)
            b2[pl.ds(b2.shape[0] - third + h * HEAD, HEAD), qc] = dot(v_t, p_bf, NN).astype(BF16)
            b1[pl.ds(h * HEAD, HEAD), qc] = dot(k_t, ds, NN).astype(BF16)
            dv += dot(do_t[:, qc], p_bf, NT)
            dk += dot(q_t[:, qc], ds, NT)
        b1[pl.ds(third + h * HEAD, HEAD), :] = dk.astype(BF16)
        b1[pl.ds(2 * third + h * HEAD, HEAD), :] = dv.astype(BF16)
    split = d - b2.shape[0]
    gacc[:, :split] += dot(x_t, b1[pl.ds(0, split), :], NT)
    gacc[:, split:] += dot(x_t, b1[pl.ds(split, d - split), :], NT) + dot(dy_t, b2[...], NT)
    acc[:, cols] += dot(wt[...], b1[...], NN)

    @pl.when(s == pl.num_programs(1) - 1)
    def _():
        for i in range(dp):
            g_ref[i, 0] = gacc[pl.ds(i * rows, rows), :]

    @pl.when(slot == pl.num_programs(0) - 1)
    def _():
        dx = dy_t.astype(F32) + acc[:, cols]
        if natural_out:
            dx_ref[0] = dx.T.astype(BF16)
        else:
            dx_ref[...] = dx.astype(BF16)


def attn_backward(pos, layer, x, dy, w, dp, natural_out):
    slots, nw, d = w.shape
    seq = x.shape[2]
    seqs = x.shape[1] // slots
    tok = seqs * seq
    nqkv = nw * 3 // 4
    last = slots - 1
    if natural_out:
        dx_shape, dx_spec = (seqs, seq, d), pl.BlockSpec((1, seq, d), lambda j, s, p: (jnp.where(j == last, s, 0), 0, 0))
    else:
        dx_shape, dx_spec = (d, tok), pl.BlockSpec((d, seq), lambda j, s, p: (0, jnp.where(j == last, s, 0)))
    return pl.pallas_call(
        functools.partial(attn_kernel, natural_out),
        out_shape=(jax.ShapeDtypeStruct(dx_shape, BF16), jax.ShapeDtypeStruct((dp, slots, d // dp, nw), F32)),
        grid_spec=pltpu.PrefetchScalarGridSpec(
            num_scalar_prefetch=1, grid=(slots, seqs),
            in_specs=[pl.BlockSpec((1, 1, seq, d), lambda j, s, p: (layer, p[0] * seqs + jnp.where(j == 0, s, seqs - 1), 0, 0)),
                      pl.BlockSpec((d, tok), lambda j, s, p: (0, 0), pipeline_mode=pl.Buffered(1)),
                      pl.BlockSpec((1, nw, d), lambda j, s, p: (j, 0, 0))],
            out_specs=[dx_spec, pl.BlockSpec((dp, 1, d // dp, nw), lambda j, s, p: (0, j, 0, 0))],
            scratch_shapes=[pltpu.VMEM((d, tok), BF16), pltpu.VMEM((d, tok), F32), pltpu.VMEM((d, nw), F32),
                            pltpu.VMEM((d, nw), BF16), pltpu.VMEM((nqkv, seq), BF16), pltpu.VMEM((nw - nqkv, seq), BF16),
                            pltpu.VMEM((nw, seq), BF16), pltpu.VMEM((256, seq), BF16)]),
        compiler_params=pltpu.CompilerParams(vmem_limit_bytes=VMEM_LIMIT, dimension_semantics=('arbitrary', 'arbitrary')),
        cost_estimate=pl.CostEstimate(flops=tok * slots * (6 * nw * d + 24 * nqkv // 3 * seq), bytes_accessed=8 * nw * d * slots, transcendentals=tok * seq * 12),
        name='attn_backward',
    )(pos, x, dy, w)


def solution(mesh):
    dp = mesh.shape['dpy'] * mesh.shape['dpx']
    act_spec = P(None, DATA_AXES, None, None)

    def scatter(g):
        n = g.shape[0] * g.shape[1]
        return lax.psum_scatter(g.reshape(n, -1, g.shape[-1]), ALL_AXES, scatter_dimension=0, tiled=True).reshape(g.shape[2:]) / dp

    def device_backward(x_saved, y_saved, dz_top, w_qkv, w_out, w_up, w_down):
        layers, d = w_up.shape[:2]
        f = w_up.shape[2]
        heads, hd = w_out.shape[1:3]
        w_a = jnp.concatenate([w_qkv.transpose(0, 2, 3, 4, 1).reshape(layers, 3 * heads * hd, d), w_out.reshape(layers, heads * hd, d)], axis=1)
        pos = lax.axis_index('tp')[None]
        w1, w2, wa = {}, {}, {}
        for l in reversed(range(layers)):
            both = lax.all_gather(jnp.stack([w_up[l], w_down[l]]), 'tp', axis=0)
            w1[l], w2[l] = both[:, 0], both[:, 1]
            wa[l] = lax.all_gather(w_a[l], 'tp', axis=0)
        grad = dz_top
        outs = {}
        for l in reversed(range(layers)):
            dy, gm = mlp_backward(pos, l, y_saved, grad, w1[l], w2[l], dp)
            outs[l, 'm'] = scatter(gm)
            grad, ga = attn_backward(pos, l, x_saved, dy, wa[l], dp, l == 0)
            outs[l, 'a'] = scatter(ga)
        d_input = lax.all_gather(grad, 'tp', axis=0, tiled=True)
        n = 3 * heads * hd
        g_a = jnp.stack([outs[l, 'a'] for l in range(layers)])
        g_m = jnp.stack([outs[l, 'm'] for l in range(layers)])
        g_qkv = g_a[:, :, :n].reshape(layers, d // dp, 3, heads, hd)
        g_out = g_a[:, :, n:].transpose(0, 2, 1).reshape(layers, heads, hd, d // dp)
        return d_input, g_qkv, g_out, g_m[:, 1], g_m[:, 0]

    return jax.shard_map(device_backward, mesh=mesh,
                         in_specs=(act_spec, act_spec, P(DATA_AXES, None, None), P(None, None, None, 'tp', None), P(None, 'tp', None, None), P(None, None, 'tp'), P(None, 'tp', None)),
                         out_specs=(P(DATA_AXES, None, None), P(None, DATA_AXES, None, 'tp', None), P(None, 'tp', None, DATA_AXES), P(None, DATA_AXES, 'tp'), P(None, ('tp', 'dpy', 'dpx'), None)),
                         check_vma=False)
```

time: 2310 us -> 867 us (0.38)
  waiting for transfers between devices: 1400 us -> 454 us
  matrix products: 720 us -> 0 us
  Pallas kernels: 0 us -> 353 us
  other arithmetic: 114 us -> 12.9 us
    psum x4 -> x0, waiting for transfers between devices: 1400 us -> none  [the longest x2 797 us: layer_backward(): lax.psum(attn_part, 'tp')]
    dot_general x28 -> x0, matrix products: 670 us -> none  [the longest x2 128 us: layer_backward(): jnp.einsum('bhqk,bqhe->bkhe', d_scores, q_heads, preferred_element_type=j...]
    pallas_call x0 -> x4, Pallas kernels: none -> 353 us  [the longest x2 227 us: attn_backward(): pl.pallas_call(functools.partial(attn_kernel, natural_out), out_shape=(ja...]
    reduce_scatter x0 -> x4, waiting for transfers between devices: none -> 313 us  [scatter(): lax.psum_scatter(g.reshape(n, -1, g.shape[-1]), ALL_AXES, scatter_dimensi...]
    all_gather x0 -> x5, waiting for transfers between devices: none -> 138 us  [the longest x1 78.8 us: device_backward(): d_input = lax.all_gather(grad, 'tp', axis=0, tiled=True)]
    convert_element_type x6 -> x0, other arithmetic: 111 us -> none  [the longest x2 54.8 us: layer_backward(): prob_bf = attn_prob.astype(jnp.bfloat16)]
    sub x2 -> x0, matrix products: 50 us -> none  [layer_backward(): attn_prob = jax.nn.softmax(scores, axis=-1)]
    unnamed x52 -> x3, local copies, waits for them, and re-layouts: 46.5 us -> 11.4 us
  transfers between devices with their start and end apart: 12 -> 9, of which waited for: 5 -> 5; matrix products, arithmetic and copies ran while one was open for 22% -> 3% of each run, Pallas kernels for 0% -> 41%
where the time goes in v2:
time: 867 us
  waiting for transfers between devices  454 us (52%)
  Pallas kernels  353 us (41%)
  local copies, waits for them, and re-layouts  32.6 us (4%)
  between operations  13.9 us (2%)
  other arithmetic  12.9 us (1%)
    reduce_scatter x4, waiting for transfers between devices, scatter(): lax.psum_scatter(g.reshape(n, -1, g.shape[-1]), ALL_AXES, scatter_dimensi...  313 us
    pallas_call x2, Pallas kernels, attn_backward(): pl.pallas_call(functools.partial(attn_kernel, natural_out), out_shape=(ja...  227 us
    pallas_call x2, Pallas kernels, mlp_backward(): pl.pallas_call(functools.partial(mlp_kernel, natural), out_shape=(jax.Sha...  127 us
    all_gather x1, waiting for transfers between devices, device_backward(): d_input = lax.all_gather(grad, 'tp', axis=0, tiled=True)  78.8 us
    all_gather x2, waiting for transfers between devices, device_backward(): both = lax.all_gather(jnp.stack([w_up[l], w_down[l]]), 'tp', axis=0)  59.3 us
  transfers between devices with their start and end apart: 9, of which 5 were waited for; matrix products, arithmetic and copies ran while one was open for 3% of the time, Pallas kernels for 41%

profile of v2, /device:TPU:0, one launch (start us, length us, event | category | flops | bytes accessed | tf_op | source)
XLA Modules:
  0.0 866.8 jit_solution(15191124236802045321)
XLA Ops:
  7.2 0.0 all-gather.14.cloned.1.call-start
  7.2 2.6 fusion.6
  9.9 1.6 pad_maximum_fusion
  11.5 0.0 copy-start
  11.5 0.0 all-gather.14.cloned.1.call-update
  11.5 0.0 all-gather.8.cloned.1.call-start
  11.5 1.0 copy-done
  12.5 3.0 pad_maximum_fusion.3
  15.5 0.0 all-gather.8.cloned.1.call-update
  15.5 0.0 all-gather.16.cloned.1.call-start
  15.6 1.6 pad_maximum_fusion.1
  17.2 0.0 all-gather.16.cloned.1.call-update
  17.3 0.0 all-gather.10.cloned.1.call-start
  17.3 0.5 all-gather.10.cloned.1.call-update
  17.8 0.0 reduce-scatter.7.cloned.1.call-start
  17.9 59.3 %all-gather.14.cloned.1.call-done = bf16[8,768,768]{2,1,0:T(8,128)(2,1)} async-done(((bf16[2,768,768]{2,1,0:T(8,128)(2,1)}), bf16[8,768,768]{2,1,0:T(8,128)(2,1)}) %all-gather.14.cloned.1.call-update) | async-done | bytes 9437200 | tf_op jit(solution)/shard_map/all_gather | solution.py:214
  77.2 8.2 slice_bitcast_fusion.2
  85.3 63.8 %mlp_backward.2 = (bf16[768,2048]{1,0:T(8,128)(2,1)}, f32[4,4,2,192,768]{4,3,2,1,0:T(8,128)}) custom-call(s32[1]{0:T(128)} %bitcast.pos_ref, bf16[2,16,512,768]{3,2,1,0:T(8,128)(2,1)} %y_ref.3, bf16[16,512,768]{2,1,0:T(8,128)(2,1)} %dz_ref.1, bf16[4,768,768]{2,1,0:T(8,128)(2,1)} %get-tuple-element.24.w1_ref, bf16[4,768,768]{2,1,0:T(8,128)(2,1)} %get-tuple-element.23.w2_ref), custom_call_target="tpu_custom_call" | custom-call | flops 48318382080 | bytes 28311552 | tf_op jit(solution)/shard_map/mlp_backward/pallas_call | solution.py:80
  149.1 0.0 all-gather.8.cloned.1.call-done.w_ref
  149.1 113.0 %attn_backward.2 = (bf16[768,2048]{1,0:T(8,128)(2,1)}, f32[4,4,192,768]{3,2,1,0:T(8,128)}) custom-call(s32[1]{0:T(128)} %bitcast.pos_ref, bf16[2,16,512,768]{3,2,1,0:T(8,128)(2,1)} %x_ref.3, bf16[768,2048]{1,0:T(8,128)(2,1)} %get-tuple-element.13.dy_ref, bf16[4,768,768]{2,1,0:T(8,128)(2,1)} %all-gather.8.cloned.1.call-done.w_ref), custom_call_target="tpu_custom_call" | custom-call | flops 48318382080 | bytes 18874368 | tf_op jit(solution)/shard_map/attn_backward/pallas_call | solution.py:180
  262.1 0.0 reduce-scatter.7.cloned.1.call-update
  262.1 0.0 reduce-scatter.5.cloned.1.call-start
  262.1 0.0 all-gather.16.cloned.1.call-done
  262.2 8.0 slice_bitcast_fusion
  270.2 62.9 %mlp_backward.3 = (bf16[768,2048]{1,0:T(8,128)(2,1)}, f32[4,4,2,192,768]{4,3,2,1,0:T(8,128)}) custom-call(s32[1]{0:T(128)} %bitcast.pos_ref, bf16[2,16,512,768]{3,2,1,0:T(8,128)(2,1)} %y_ref.3, bf16[768,2048]{1,0:T(8,128)(2,1)} %get-tuple-element.14.dz_ref, bf16[4,768,768]{2,1,0:T(8,128)(2,1)} %get-tuple-element.22.w1_ref, ...), custom_call_target="tpu_custom_call" | custom-call | flops 48318382080 | bytes 28311552 | tf_op jit(solution)/shard_map/mlp_backward/pallas_call | solution.py:80
  333.1 0.0 all-gather.10.cloned.1.call-done.w_ref
  333.1 113.7 %attn_backward.3 = (bf16[4,512,768]{2,1,0:T(8,128)(2,1)}, f32[4,4,192,768]{3,2,1,0:T(8,128)}) custom-call(s32[1]{0:T(128)} %bitcast.pos_ref, bf16[2,16,512,768]{3,2,1,0:T(8,128)(2,1)} %x_ref.3, bf16[768,2048]{1,0:T(8,128)(2,1)} %get-tuple-element.15.dy_ref, bf16[4,768,768]{2,1,0:T(8,128)(2,1)} %all-gather.10.cloned.1.call-done.w_ref), custom_call_target="tpu_custom_call" | custom-call | flops 48318382080 | bytes 18874368 | tf_op jit(solution)/shard_map/attn_backward/pallas_call | solution.py:180
  446.8 0.0 reduce-scatter.5.cloned.1.call-update
  446.8 0.0 all-gather.12.cloned.1.call-start
  446.9 0.7 all-gather.12.cloned.1.call-update
  447.6 0.0 reduce-scatter.11.cloned.1.call-start
  447.6 0.7 reduce-scatter.11.cloned.1.call-update
  448.3 0.0 reduce-scatter.9.cloned.1.call-start
  448.4 0.7 reduce-scatter.9.cloned.1.call-update
  449.1 0.0 reduce-scatter.7.cloned.1.call-done
  449.1 1.1 broadcast_multiply_fusion.2
  450.2 76.3 %reduce-scatter.5.cloned.1.call-done = f32[1,192,768]{2,1,0:T(8,128)} async-done(((f32[16,192,768]{2,1,0:T(8,128)}), f32[1,192,768]{2,1,0:T(8,128)}) %reduce-scatter.5.cloned.1.call-update) | async-done | bytes 589840 | tf_op jit(solution)/shard_map/reduce_scatter | solution.py:204
  526.5 1.1 broadcast_multiply_fusion.3
  527.6 0.2 fusion.5
  527.7 0.9 copy.25
  528.7 0.1 fusion.4
  528.7 1.4 copy.24
  530.1 78.8 %all-gather.12.cloned.1.call-done = bf16[16,512,768]{2,1,0:T(8,128)(2,1)} async-done(((bf16[4,512,768]{2,1,0:T(8,128)(2,1)}), bf16[16,512,768]{2,1,0:T(8,128)(2,1)}) %all-gather.12.cloned.1.call-update) | async-done | bytes 12582928 | tf_op jit(solution)/shard_map/all_gather | solution.py:224
  608.9 119.0 %reduce-scatter.11.cloned.1.call-done = f32[1,384,768]{2,1,0:T(8,128)} async-done(((f32[16,384,768]{2,1,0:T(8,128)}), f32[1,384,768]{2,1,0:T(8,128)}) %reduce-scatter.11.cloned.1.call-update) | async-done | bytes 1179664 | tf_op jit(solution)/shard_map/reduce_scatter | solution.py:204
  727.9 1.3 broadcast_multiply_fusion
  729.3 117.7 %reduce-scatter.9.cloned.1.call-done = f32[1,384,768]{2,1,0:T(8,128)} async-done(((f32[16,384,768]{2,1,0:T(8,128)}), f32[1,384,768]{2,1,0:T(8,128)}) %reduce-scatter.9.cloned.1.call-update) | async-done | bytes 1179664 | tf_op jit(solution)/shard_map/reduce_scatter | solution.py:204
  846.9 1.3 broadcast_multiply_fusion.1
  848.3 1.6 fusion.3
  849.8 10.4 %copy.31 = bf16[16,512,768]{2,1,0:T(8,128)(2,1)} copy(bf16[16,512,768]{2,1,0:T(8,128)(2,1)} %all-gather.12.cloned.1.call-done) | data formatting | bytes 25165824
Async XLA Ops:
  7.2 70.0 %all-gather.14.cloned.1.call-start = ((), (), s32[]{:S(2)}) async-start(), calls=%async_computation.11 | async-start | bytes 11796480 | tf_op jit(solution)/shard_map/all_gather | solution.py:214
  11.5 1.1 copy-start
  11.5 137.6 %all-gather.8.cloned.1.call-start = ((), (), s32[]{:S(2)}) async-start(), calls=%async_computation.4 | async-start | bytes 5898240 | tf_op jit(solution)/shard_map/all_gather | solution.py:216
  15.5 246.6 %all-gather.16.cloned.1.call-start = ((), (), s32[]{:S(2)}) async-start(), calls=%async_computation.12 | async-start | bytes 11796480 | tf_op jit(solution)/shard_map/all_gather | solution.py:214
  17.3 315.8 %all-gather.10.cloned.1.call-start = ((), (), s32[]{:S(2)}) async-start(), calls=%async_computation.5 | async-start | bytes 5898240 | tf_op jit(solution)/shard_map/all_gather | solution.py:216
  17.8 431.3 %reduce-scatter.7.cloned.1.call-start = ((), (), s32[]{:S(2)}) async-start(), calls=%async_computation.8 | async-start | bytes 10027008 | tf_op jit(solution)/shard_map/reduce_scatter | solution.py:204
  262.1 264.4 %reduce-scatter.5.cloned.1.call-start = ((), (), s32[]{:S(2)}) async-start(), calls=%async_computation.7 | async-start | bytes 10027008 | tf_op jit(solution)/shard_map/reduce_scatter | solution.py:204
  446.8 162.1 %all-gather.12.cloned.1.call-start = ((), (), s32[]{:S(2)}) async-start(), calls=%async_computation.6 | async-start | bytes 15728640 | tf_op jit(solution)/shard_map/all_gather | solution.py:224
  447.6 280.3 %reduce-scatter.11.cloned.1.call-start = ((), (), s32[]{:S(2)}) async-start(), calls=%async_computation.10 | async-start | bytes 20054016 | tf_op jit(solution)/shard_map/reduce_scatter | solution.py:204
  448.3 398.6 %reduce-scatter.9.cloned.1.call-start = ((), (), s32[]{:S(2)}) async-start(), calls=%async_computation.9 | async-start | bytes 20054016 | tf_op jit(solution)/shard_map/reduce_scatter | solution.py:204
Sparse Core Ops, SparseCore 0:
  11.6 65.5 all-gather.13
  79.3 35.4 all-gather.7
  116.3 62.6 all-gather.15
  181.0 35.4 all-gather.9
  262.2 79.4 reduce-scatter.6
  447.0 79.4 reduce-scatter.4
  528.0 80.8 all-gather.11
  613.8 114.0 reduce-scatter.10
  732.8 114.0 reduce-scatter.8

commit v3 on v0

v3 whole, which is shorter than its diff:
```python
import functools
import math

import jax
import jax.numpy as jnp
from jax import lax
from jax.experimental import pallas as pl
from jax.experimental.pallas import tpu as pltpu
from jax.sharding import PartitionSpec as P

DATA_AXES = ('dpy', 'dpx')
F32 = jnp.float32
BF16 = jnp.bfloat16
HEAD = 64
SLOTS = 4
NN = (((1,), (0,)), ((), ()))
NT = (((1,), (1,)), ((), ()))
VMEM_LIMIT = 63 * 1024 * 1024
MESH = pl.DeviceIdType.MESH
ANY = pl.BlockSpec(memory_space=pl.ANY)


def dot(a, b, dims):
    return lax.dot_general(a, b, dims, preferred_element_type=F32)


class Peers:
    def __init__(self):
        z, y, t = lax.axis_index('dpy'), lax.axis_index('dpx'), lax.axis_index('tp')
        self.z, self.y, self.t = z, y, t
        self.sib = (z, y, t + 1 - 2 * (t % 2))
        self.xp = (z, y, (t + 2) % 4)
        self.yp = (z, 1 - y, t)
        self.zp = (1 - z, y, t)

    def barrier(self):
        sem = pltpu.get_barrier_semaphore()
        for peer in (self.sib, self.xp, self.yp, self.zp):
            pl.semaphore_signal(sem, inc=1, device_id=peer, device_id_type=MESH)
        pl.semaphore_wait(sem, 4)

    def rel(self, d):
        zr = self.z if d // 2 == 0 else 1 - self.z
        yr = self.y if d % 2 == 0 else 1 - self.y
        return zr * 2 + yr


class Sems:
    def __init__(self, send, recv, local):
        self.send, self.recv, self.local = send, recv, local
        self.n = self.m = 0

    def remote(self, src, dst, peer):
        i = self.n
        self.n += 1
        return lambda: pltpu.make_async_remote_copy(src_ref=src(), dst_ref=dst(), send_sem=self.send.at[i], recv_sem=self.recv.at[i],
                                                    device_id=peer, device_id_type=MESH)

    def copy(self, src, dst):
        i = self.m
        self.m += 1
        return lambda: pltpu.make_async_copy(src(), dst(), self.local.at[i])


def at_ticks(actions, tick, position=0, points=1):
    for k in sorted(actions):
        if k % points == position:
            @pl.when(tick == k)
            def _(k=k):
                for action in actions[k]:
                    action()


class Scatter:
    def __init__(self, sems, peers, partial, mine, bufs, out, rows, load=True):
        r0, r1, r2, r3 = self.bufs = bufs
        first, count = rows
        h = count // 2
        self.mine, self.all, self.lo, self.hi = mine, pl.ds(first, count), pl.ds(first, h), pl.ds(first + h, h)
        self.half = half = pl.ds(first // 2, h)
        every, lo, hi = self.all, self.lo, self.hi
        self.load, self.c0, self.c1, self.c2 = [], [], [], []
        for x in range(2):
            def near(k, part, x=x):
                return lambda: mine(x).at[k, part]

            def place(buf, *index):
                return lambda: buf.at[index]
            if load:
                self.load.append(sems.copy(lambda x=x: partial(2 * x).at[:, every], near(slice(None), every)))
            self.c0.append(sems.remote(lambda x=x: partial(2 * x + 1).at[:, every], place(r0, x, slice(None), every), peers.sib))
            self.c1.append([sems.remote(near(2 * k + 1, lo), place(r1, 0, x, k, half), peers.yp) for k in range(2)]
                           + [sems.remote(near(2 + k, hi), place(r1, 1, x, k, half), peers.zp) for k in range(2)])
            self.c2.append([sems.remote(near(2, lo), place(r2, 0, x, half), peers.zp), sems.remote(near(1, hi), place(r2, 1, x, half), peers.yp)])
        self.c3 = sems.remote(lambda: mine(1).at[0, every], place(r3, every), peers.xp)
        self.store = sems.copy(lambda: mine(0).at[0, every], out)

    def start(self, x):
        self.c0[x]().start()
        if self.load:
            self.load[x]().start()

    def add0(self, x):
        if self.load:
            self.load[x]().wait()
        self.c0[x]().wait_recv()
        mine, r0 = self.mine(x), self.bufs[0].at[x]

        def body(k, carry):
            mine[k, self.all] = mine[k, self.all] + r0[k, self.all]
            return carry
        lax.fori_loop(0, 4, body, 0)

    def send1(self, x):
        for c in self.c1[x]:
            c().start()

    def add1(self, x):
        for c in self.c1[x]:
            c().wait_recv()
        mine, r1 = self.mine(x), self.bufs[1]

        def body(k, carry):
            mine[2 * k, self.lo] = mine[2 * k, self.lo] + r1[0, x, k, self.half]
            mine[k, self.hi] = mine[k, self.hi] + r1[1, x, k, self.half]
            return carry
        lax.fori_loop(0, 2, body, 0)

    def send2(self, x):
        for c in self.c2[x]:
            c().start()

    def add2(self, x):
        for c in self.c2[x]:
            c().wait_recv()
        mine, r2 = self.mine(x), self.bufs[2]
        mine[0, self.lo] = mine[0, self.lo] + r2[0, x, self.half]
        mine[0, self.hi] = mine[0, self.hi] + r2[1, x, self.half]

    def send3(self):
        self.c3().start()

    def add3(self):
        self.c3().wait_recv()
        mine = self.mine(0)
        mine[0, self.all] = (mine[0, self.all] + self.bufs[3][self.all]) * (1 / SLOTS)

    def out(self):
        self.store().start()

    def finish(self):
        for c in self.c0 + sum(self.c1, []) + sum(self.c2, []) + [self.c3]:
            c().wait_send()
        self.store().wait()

    def both(self, name):
        for x in range(2):
            getattr(self, name)(x)


def scatter_bufs(rows, d):
    return [pltpu.VMEM((2, 4, rows, d), F32), pltpu.VMEM((2, 2, 2, rows // 2, d), F32), pltpu.VMEM((2, 2, rows // 2, d), F32), pltpu.VMEM((rows, d), F32)]


def steps(job, plan):
    out = []
    for k, name in plan:
        out.append((k, functools.partial(job.both, name) if name[-1] in '012' or name == 'start' else getattr(job, name)))
    return out


class Gather:
    def __init__(self, sems, peers, blocks):
        self.sib = [sems.remote(own, lambda dst=dst: dst(1), peers.sib) for own, dst in blocks]
        self.xp = [sems.remote(own, lambda dst=dst: dst(2), peers.xp) for own, dst in blocks]
        self.fwd = [sems.remote(lambda dst=dst: dst(2), lambda dst=dst: dst(3), peers.sib) for own, dst in blocks]

    def start(self, blocks):
        for i in blocks:
            self.sib[i]().start()
            self.xp[i]().start()

    def forward(self, i):
        self.xp[i]().wait_recv()
        self.fwd[i]().start()

    def finish(self, sib=True):
        for i in range(len(self.sib)):
            if sib:
                self.sib[i]().wait_recv()
                self.fwd[i]().wait_recv()
            self.sib[i]().wait_send()
            self.xp[i]().wait_send()
            self.fwd[i]().wait_send()


class Bounce:
    def __init__(self, sems, items, buf):
        self.steps = []
        prev = None
        for own, dst, rows in items:
            ld = sems.copy(own, lambda rows=rows: buf.at[pl.ds(0, rows)])
            st = sems.copy(lambda rows=rows: buf.at[pl.ds(0, rows)], lambda dst=dst: dst(0))
            self.steps.append(functools.partial(self.load, prev, ld))
            self.steps.append(functools.partial(self.flip, ld, st))
            prev = st
        self.steps.append(lambda prev=prev: prev().wait())

    @staticmethod
    def load(prev, ld):
        if prev is not None:
            prev().wait()
        ld().start()

    @staticmethod
    def flip(ld, st):
        ld().wait()
        st().start()


def merge(*lists):
    actions = {}
    for pairs in lists:
        for k, action in pairs:
            actions.setdefault(k, []).append(action)
    return actions


SEMS = [pltpu.SemaphoreType.DMA((96,)), pltpu.SemaphoreType.DMA((96,)), pltpu.SemaphoreType.DMA((24,))]


def whole(*shape):
    return pl.BlockSpec(shape, lambda *_: (0,) * len(shape), pipeline_mode=pl.Buffered(1))


def leading(*shape):
    return pl.BlockSpec((1,) + shape, lambda j, *_: (j,) + (0,) * len(shape))


def params(collective_id, axes):
    return pltpu.CompilerParams(vmem_limit_bytes=VMEM_LIMIT, dimension_semantics=('arbitrary',) * axes, collective_id=collective_id, has_side_effects=True)


def mlp_slot(seqs, seq, w1, w2, w1t, yt, dz, acc, gt, dht, tick):
    w1t[...] = w1[...].T

    def block(i, carry):
        tick(i)
        cols = pl.ds(pl.multiple_of(i * seq, seq), seq)
        h = dot(w1t[...], yt[:, cols], NN)
        dg = dot(w2[...], dz[:, cols], NN)
        c0 = math.sqrt(2 / math.pi)
        c1 = 0.044715 * c0
        h2 = h * h
        t = jnp.tanh(h * (c0 + c1 * h2))
        q = 0.5 * t + 0.5
        g = h * q
        dh = dg * (q + (g * (1.0 - t)) * (c0 + (3 * c1) * h2))
        gt[:, cols] = g.astype(BF16)
        dh = dh.astype(BF16)
        dht[:, cols] = dh
        acc[:, cols] += dot(w1[...], dh, NN)
        return carry
    lax.fori_loop(0, seqs, block, 0)


def store_shards(peers, g_ref, j, g):
    rows = g_ref.shape[-2]
    for d in range(4):
        g_ref[0, j, peers.rel(d)] = g[d * rows:(d + 1) * rows]


def mlp_rest(slot, actions, peers, seqs, seq, w1, w2, dz, dy_ref, g_ref, w1t, yt, acc, gt, dht):
    points = seqs + 2
    first = slot * points

    def tick(i):
        at_ticks({k: v for k, v in actions.items() if k % points < seqs}, first + i)
    mlp_slot(seqs, seq, w1, w2, w1t, yt, dz, acc, gt, dht, tick)
    at_ticks(actions, first + seqs, seqs, points)
    store_shards(peers, g_ref, 0, dot(gt[...], dz[...], NT))
    at_ticks(actions, first + seqs + 1, seqs + 1, points)
    store_shards(peers, g_ref, 1, dot(yt[...], dht[...], NT))

    @pl.when(slot == SLOTS - 1)
    def _():
        dy_ref[...] = (dz[...].astype(F32) + acc[...]).astype(BF16)


def attn_weights(layer, wq, wo, wa_g):
    nq, d = wq.shape[1:]
    return [(lambda: wq.at[layer], lambda j: wa_g.at[j, pl.ds(0, nq)], nq), (lambda: wo.at[layer], lambda j: wa_g.at[j, pl.ds(nq, d - nq)], d - nq)]


class Spread:
    def __init__(self, sems, peers, wb, pieces):
        rows = wb.shape[2] // pieces
        y = peers.y

        def piece(slot, m, k):
            return lambda: wb.at[slot, m, pl.ds(k * rows, rows)]
        every = range(pieces)
        self.sib = sems.remote(lambda: wb.at[0], lambda: wb.at[1], peers.sib)
        self.xp = [sems.remote(piece(0, y, k), piece(2, y, k), peers.xp) for k in every]
        self.fy, self.wy = [], []
        for k in every:
            self.fy.append(sems.remote(piece(2, y, k), piece(2, y, k), peers.yp))
            sems.n -= 1
            self.wy.append(sems.remote(piece(2, 1 - y, k), piece(2, 1 - y, k), peers.yp))
        self.fs = [sems.remote(piece(2, y, k), piece(3, y, k), peers.sib) for k in every]
        self.fs2 = [sems.remote(piece(2, 1 - y, k), piece(3, 1 - y, k), peers.sib) for k in every]

    def start(self):
        for c in self.xp + [self.sib]:
            c().start()

    def forward(self, k):
        self.xp[k]().wait_recv()
        self.fy[k]().start()
        self.fs[k]().start()

    def forward2(self, k):
        self.wy[k]().wait_recv()
        self.fs2[k]().start()

    def arrived(self):
        for c in self.fs + self.fs2:
            c().wait_recv()

    def finish(self):
        for c in [self.sib] + self.xp + self.fy + self.fs + self.fs2:
            c().wait_send()


def mlp_first_kernel(layer, y_ref, dz_ref, wup, wdn, wq, wo, dy_ref, g_ref, wa_g, yt, dzt, acc, w1t, gt, dht, wb, bounce, *rest):
    slot = pl.program_id(0)
    seqs, seq = y_ref.shape[1:3]
    peers, sems = Peers(), Sems(*rest)
    own = [sems.copy(lambda w=w: w.at[layer], lambda m=m: wb.at[0, m]) for m, w in enumerate((wup, wdn))]
    blocks = attn_weights(layer, wq, wo, wa_g)
    gather = Gather(sems, peers, [r[:2] for r in blocks])
    hop = Bounce(sems, blocks, bounce)
    spread = Spread(sems, peers, wb, SLOTS)

    @pl.when(slot == 0)
    def _():
        for c in own:
            c().start()
        peers.barrier()
        for c in own:
            c().wait()
        spread.start()
        gather.start(range(2))
        acc[...] = jnp.zeros_like(acc)
        for s in range(seqs):
            cols = slice(s * seq, (s + 1) * seq)
            yt[:, cols] = y_ref[0, s].T
            dzt[:, cols] = dz_ref[s].T

    @pl.when(slot == 1)
    def _():
        spread.sib().wait_recv()

    @pl.when(slot == 2)
    def _():
        spread.forward2(2)
        spread.forward2(3)

    @pl.when(slot == 3)
    def _():
        spread.arrived()
    ahead = [(4, 0), (6, 1), (8, 2), (11, 3)]
    actions = merge([(14 + k, s) for k, s in enumerate(hop.steps)], [(t, functools.partial(spread.forward, k)) for t, k in ahead],
                    [(7, functools.partial(spread.forward2, 0)), (10, functools.partial(spread.forward2, 1)), (21, functools.partial(gather.forward, 0))])
    mlp_rest(slot, actions, peers, seqs, seq, wb.at[slot, 0], wb.at[slot, 1], dzt, dy_ref, g_ref, w1t, yt, acc, gt, dht)

    @pl.when(slot == SLOTS - 1)
    def _():
        gather.forward(1)
        spread.finish()
        gather.finish()


def mlp_first(layer, y, dz, wup, wdn, wq, wo):
    d, f = wup.shape[1:]
    seq = y.shape[2]
    seqs = y.shape[1] // SLOTS
    tok = seqs * seq
    once = pl.Buffered(1)
    return pl.pallas_call(
        functools.partial(mlp_first_kernel, layer),
        out_shape=(jax.ShapeDtypeStruct((d, tok), BF16), jax.ShapeDtypeStruct((SLOTS, 2, 4, d // 4, f), F32), jax.ShapeDtypeStruct((SLOTS, d, d), BF16)),
        grid=(SLOTS,),
        in_specs=[pl.BlockSpec((1, seqs, seq, d), lambda j: (layer, lax.axis_index('tp'), 0, 0), pipeline_mode=once),
                  pl.BlockSpec((seqs, seq, d), lambda j: (lax.axis_index('tp'), 0, 0), pipeline_mode=once), ANY, ANY, ANY, ANY],
        out_specs=[whole(d, tok), leading(2, 4, d // 4, f), ANY],
        scratch_shapes=[pltpu.VMEM((d, tok), BF16), pltpu.VMEM((d, tok), BF16), pltpu.VMEM((d, tok), F32), pltpu.VMEM((f, d), BF16),
                        pltpu.VMEM((f, tok), BF16), pltpu.VMEM((f, tok), BF16), pltpu.VMEM((SLOTS, 2, d, f), BF16), pltpu.VMEM((d, d), BF16)] + SEMS,
        compiler_params=params(0, 1),
        name='mlp_first',
    )(y, dz, wup, wdn, wq, wo)


def mlp_second_kernel(layer, y_ref, dz_ref, w1_ref, w2_ref, partial, wq, wo, dy_ref, g_ref, wa_g, red, yt, acc, w1t, gt, dht, bounce, mine, *rest):
    slot = pl.program_id(0)
    seqs, seq = y_ref.shape[1:3]
    bufs, rest = rest[:4], rest[4:]
    peers, sems = Peers(), Sems(*rest)
    blocks = attn_weights(layer, wq, wo, wa_g)
    gather = Gather(sems, peers, [r[:2] for r in blocks])
    hop = Bounce(sems, blocks, bounce)
    rows = mine.shape[2] // 2
    a, b = jobs = [Scatter(sems, peers, lambda s: partial.at[s], lambda x: mine.at[x], bufs, lambda j=j: red.at[pl.ds(j * rows, rows)], (j * rows, rows)) for j in range(2)]

    @pl.when(slot == 0)
    def _():
        peers.barrier()
        for job in jobs:
            job.both('start')
        gather.start(range(2))
        acc[...] = jnp.zeros_like(acc)
        for s in range(seqs):
            yt[:, slice(s * seq, (s + 1) * seq)] = y_ref[0, s].T
    actions = merge([(4 + k, s) for k, s in enumerate(hop.steps)], [(11, functools.partial(gather.forward, 0)), (12, functools.partial(gather.forward, 1))],
                    steps(a, [(3, 'add0'), (4, 'send1'), (10, 'add1'), (11, 'send2'), (17, 'add2'), (18, 'send3'), (22, 'add3'), (23, 'out')]),
                    steps(b, [(4, 'add0'), (5, 'send1'), (15, 'add1'), (16, 'send2'), (20, 'add2'), (21, 'send3')]))
    mlp_rest(slot, actions, peers, seqs, seq, w1_ref.at[0], w2_ref.at[0], dz_ref, dy_ref, g_ref, w1t, yt, acc, gt, dht)

    @pl.when(slot == SLOTS - 1)
    def _():
        b.add3()
        gather.finish()
        b.out()
        a.finish()
        b.finish()


def mlp_second(layer, y, dz, w1, w2, partial, wq, wo):
    d, f = w1.shape[1:]
    seq = y.shape[2]
    seqs = y.shape[1] // SLOTS
    tok = seqs * seq
    return pl.pallas_call(
        functools.partial(mlp_second_kernel, layer),
        out_shape=(jax.ShapeDtypeStruct((d, tok), BF16), jax.ShapeDtypeStruct((SLOTS, 2, 4, d // 4, f), F32), jax.ShapeDtypeStruct((SLOTS, d, d), BF16),
                   jax.ShapeDtypeStruct((d // 4, d), F32)),
        grid=(SLOTS,),
        in_specs=[pl.BlockSpec((1, seqs, seq, d), lambda j: (layer, lax.axis_index('tp'), 0, 0), pipeline_mode=pl.Buffered(1)),
                  whole(d, tok), leading(d, f), leading(f, d), ANY, ANY, ANY],
        out_specs=[whole(d, tok), leading(2, 4, d // 4, f), ANY, ANY],
        scratch_shapes=[pltpu.VMEM((d, tok), BF16), pltpu.VMEM((d, tok), F32), pltpu.VMEM((f, d), BF16),
                        pltpu.VMEM((f, tok), BF16), pltpu.VMEM((f, tok), BF16), pltpu.VMEM((d, d), BF16), pltpu.VMEM((2, 4, d // 4, d), F32)]
        + scatter_bufs(d // 4, d) + SEMS,
        compiler_params=params(1, 1),
        name='mlp_second',
    )(y, dz, w1, w2, partial, wq, wo)


def attn_step(peers, x_ref, dy_ref, w_ref, xt, acc, gacc, qkv, do, b1, b2, emit):
    s, slot = pl.program_id(0), pl.program_id(1)
    step = s * SLOTS + slot
    last = SLOTS * SLOTS - 1
    before = (step + last) % (last + 1)
    seq, d = x_ref.shape[-2:]
    nqkv = qkv.shape[0]
    third = nqkv // 3
    split = d - b2.shape[1]
    rows = d // 4

    def tokens(n):
        return pl.ds(pl.multiple_of(n * seq, seq), seq)

    @pl.when(step == 0)
    def _():
        xt[1] = jnp.zeros((d, seq), BF16)
        for j in range(SLOTS):
            gacc[j] = jnp.zeros(gacc.shape[1:], F32)
        for j in range(2):
            b1[j] = jnp.zeros(b1.shape[1:], BF16)
            b2[j] = jnp.zeros(b2.shape[1:], BF16)

    @pl.when(slot == 0)
    def _():
        xt[s % 2] = x_ref[0, 0].T

    def grads(n):
        ps, pj, par = n // SLOTS, n % SLOTS, n % 2
        third_d = d // 3

        def weights(c):
            cols = slice(c * third_d, (c + 1) * third_d)
            g = dot(xt[ps % 2], b1[par, cols], NT)
            if c == 2:
                g = g + dot(dy_ref[:, tokens(ps)], b2[par], NT)
            for k in range(4):
                r = peers.rel(k)
                gacc[pj, r, :, cols] = gacc[pj, r, :, cols] + g[k * rows:(k + 1) * rows]

        def inputs(c):
            part = slice(c * third_d, (c + 1) * third_d)
            acc[part] += dot(w_ref[pj, :, part].T, b1[par], NN)
        return [functools.partial(f, c) for c in range(3) for f in (weights, inputs)]
    x_t = xt[s % 2]
    dy_t = dy_ref[:, tokens(s)]
    now = step % 2
    qkv[...] = dot(w_ref[slot, pl.ds(0, nqkv), :], x_t, NN).astype(BF16)
    do[...] = dot(w_ref[slot, pl.ds(nqkv, d - nqkv), :], dy_t, NN).astype(BF16)
    scale = HEAD ** -0.5
    exp_scale = scale * math.log2(math.e)
    qb = seq // 2
    units = [(h, slice(c * qb, (c + 1) * qb)) for h in range(third // HEAD) for c in range(2)]

    def scores(h, qc):
        q_rows, k_rows, v_rows = head_rows(h)
        return dot(qkv[k_rows, :].T, qkv[q_rows, qc], NN), dot(qkv[v_rows, :].T, do[q_rows, qc] * scale, NN)

    def head_rows(h):
        return [slice(i * third + h * HEAD, i * third + (h + 1) * HEAD) for i in range(3)]
    ahead = scores(*units[0])
    pieces = grads(before)
    for n, (h, qc) in enumerate(units):
        sc, dp_t = ahead
        if n + 1 < len(units):
            ahead = scores(*units[n + 1])
        pieces[n]()
        q_rows, k_rows, v_rows = head_rows(h)
        m = jnp.max(sc, axis=0, keepdims=True)
        e = jnp.exp2((sc - m) * exp_scale)
        inv = 1.0 / jnp.sum(e, axis=0, keepdims=True)
        rd = jnp.sum(e * dp_t, axis=0, keepdims=True) * inv
        p = e * inv
        p_bf = p.astype(BF16)
        ds = (p * (dp_t - rd)).astype(BF16)
        b2[now, pl.ds(b2.shape[1] - third + h * HEAD, HEAD), qc] = dot(qkv[v_rows, :], p_bf, NN).astype(BF16)
        b1[now, q_rows, qc] = dot(qkv[k_rows, :], ds, NN).astype(BF16)
        dv_c = dot(do[q_rows, qc], p_bf, NT)
        dk_c = dot(qkv[q_rows, qc], ds, NT)
        if n % 2 == 0:
            dv, dk = dv_c, dk_c
        else:
            b1[now, k_rows] = (dk + dk_c).astype(BF16)
            b1[now, v_rows] = (dv + dv_c).astype(BF16)

    @pl.when(slot == 0)
    def _():
        @pl.when(s > 0)
        def _():
            emit(s - 1)
        acc[...] = dy_ref[:, tokens(s)].astype(F32)

    @pl.when(step == last)
    def _():
        for piece in grads(last):
            piece()
        emit(s)


ATTN_IN = 3
ATTN_SCRATCH = 7
JOB_PLAN = [(2, 'add0'), (3, 'send1'), (9, 'add1'), (10, 'send2')], [(3, 'add0'), (4, 'send1'), (14, 'add1'), (15, 'send2')]


def attn_first_kernel(layer, x_ref, dy_ref, w_ref, partial, wup, wdn, dx_ref, g_hbm, w1_g, w2_g, red, *rest):
    body, rest = rest[:ATTN_SCRATCH], rest[ATTN_SCRATCH:]
    gacc, mine, bounce = body[2], rest[:2], rest[-4]
    seq = x_ref.shape[-2]
    step = pl.program_id(0) * SLOTS + pl.program_id(1)
    peers, sems = Peers(), Sems(*rest[-3:])
    a, b = jobs = [Scatter(sems, peers, lambda s, j=j: partial.at[s, j], lambda x, j=j: mine[j].at[x], rest[2 + 4 * j:6 + 4 * j], lambda j=j: red.at[j],
                           (0, red.shape[1])) for j in range(2)]
    blocks = [(lambda w=w: w.at[layer - 1], lambda j, g=g: g.at[j], wup.shape[1]) for w, g in ((wup, w1_g), (wdn, w2_g))]
    gather = Gather(sems, peers, [r[:2] for r in blocks])
    hop = Bounce(sems, blocks, bounce)
    stores = [sems.copy(lambda j=j: gacc.at[j], lambda j=j: g_hbm.at[j]) for j in range(SLOTS)]
    actions = merge(steps(a, JOB_PLAN[0]), steps(b, JOB_PLAN[1]), [(5 + k, s) for k, s in enumerate(hop.steps)],
                    [(7, functools.partial(gather.forward, 0)), (13, functools.partial(gather.forward, 1))])

    @pl.when(step == 0)
    def _():
        peers.barrier()
        for job in jobs:
            job.both('start')
        gather.start(range(2))
    at_ticks(actions, step)

    def emit(s):
        dx_ref[:, pl.ds(pl.multiple_of(s * seq, seq), seq)] = acc[...].astype(BF16)
    acc = body[1]
    attn_step(peers, x_ref, dy_ref, w_ref, *body, emit)

    @pl.when(step == SLOTS * SLOTS - 1)
    def _():
        for job in jobs:
            job.both('add2')
            job.send3()
        for c in stores:
            c().start()
        gather.finish()
        for job in jobs:
            job.add3()
        for job in jobs:
            job.out()
        for c in stores:
            c().wait()
        for job in jobs:
            job.finish()


def attn_last_kernel(x_ref, dy_ref, w_ref, partial, dxg, red, red_last, *rest):
    body, rest = rest[:ATTN_SCRATCH], rest[ATTN_SCRATCH:]
    acc, gacc, mine, dxb, free = body[1], body[2], rest[:2], rest[-5], rest[-4]
    step = pl.program_id(0) * SLOTS + pl.program_id(1)
    seqs = pl.num_programs(0)
    peers, sems = Peers(), Sems(*rest[-3:])
    nred = red.shape[1]
    a, b = jobs = [Scatter(sems, peers, lambda s, j=j: partial.at[s, j], lambda x, j=j: mine[j].at[x], rest[2 + 4 * j:6 + 4 * j], lambda j=j: red.at[j],
                           (0, nred)) for j in range(2)]
    h = nred // 2
    ends = [Scatter(sems, peers, lambda s: gacc.at[s], lambda x: gacc.at[2 * x], rest[2:6], lambda j=j: red_last.at[pl.ds(j * h, h)], (j * h, h), load=False)
            for j in range(2)]
    t = peers.t
    t2 = (t + 2) % SLOTS
    sib, xp, fwd, mine_dx = [], [], [], []
    for s in range(SLOTS):
        def src(s=s):
            return dxb.at[s]

        def dst(s=s):
            return dxg.at[t * SLOTS + s]

        def other(s=s):
            return dxg.at[t2 * SLOTS + s]
        mine_dx.append(sems.copy(src, dst))
        sib.append(sems.remote(src, dst, peers.sib))
        xp.append(sems.remote(src, dst, peers.xp))
        fwd.append(sems.remote(other, other, peers.sib))

    def freed(i, who):
        for peer in who:
            pl.semaphore_signal(free.at[i], inc=1, device_id=peer, device_id_type=MESH)

    def forward(s):
        xp[s]().wait_recv()
        fwd[s]().start()
    actions = merge(steps(a, JOB_PLAN[0]), steps(b, JOB_PLAN[1]), [(3, lambda: freed(0, [peers.sib])), (10, lambda: freed(1, [peers.yp, peers.zp])),
                                                                  (10, functools.partial(forward, 0)), (14, functools.partial(forward, 1))])

    @pl.when(step == 0)
    def _():
        peers.barrier()
        for job in jobs:
            job.both('start')
    at_ticks(actions, step)

    def emit(s):
        dxb[s] = acc[...].T.astype(BF16)
        for k in range(SLOTS):
            @pl.when(s == k)
            def _(k=k):
                for c in (xp, sib, mine_dx):
                    c[k]().start()
    attn_step(peers, x_ref, dy_ref, w_ref, *body, emit)

    @pl.when(step == SLOTS * SLOTS - 1)
    def _():
        pl.semaphore_wait(free.at[0], 1)
        for job in ends:
            job.both('start')
        a.both('add2')
        a.send3()
        freed(2, [peers.yp, peers.zp])
        pl.semaphore_wait(free.at[1], 2)
        for job in ends:
            job.both('add0')
        for job in ends:
            job.both('send1')
        forward(2)
        b.both('add2')
        b.send3()
        a.add3()
        freed(3, [peers.xp])
        pl.semaphore_wait(free.at[2], 2)
        for job in ends:
            job.both('add1')
            job.both('send2')
        pl.semaphore_wait(free.at[3], 1)
        forward(3)
        a.out()
        b.add3()
        b.out()
        for job in ends:
            job.both('add2')
            job.send3()
        for s in range(SLOTS):
            mine_dx[s]().wait()
            sib[s]().wait()
            xp[s]().wait_send()
        for job in ends:
            job.add3()
        for job in ends:
            job.out()
        for s in range(SLOTS):
            fwd[s]().wait()
        for job in jobs + ends:
            job.finish()


def attn_specs(layer, x, w):
    slots, nw, d = w.shape
    seq = x.shape[2]
    seqs = x.shape[1] // slots
    tok = seqs * seq
    nqkv = nw * 3 // 4
    in_specs = [pl.BlockSpec((1, 1, seq, d), lambda s, j: (layer, lax.axis_index('tp') * seqs + s, 0, 0)), whole(d, tok), whole(slots, nw, d), ANY]
    scratch = [pltpu.VMEM((2, d, seq), BF16), pltpu.VMEM((d, seq), F32), pltpu.VMEM((slots, 4, d // 4, nw), F32), pltpu.VMEM((nqkv, seq), BF16),
               pltpu.VMEM((nw - nqkv, seq), BF16), pltpu.VMEM((2, nw, seq), BF16), pltpu.VMEM((2, d // 3, seq), BF16)]
    scratch += [pltpu.VMEM((2, 4, d // 4, d), F32)] * 2 + scatter_bufs(d // 4, d) * 2
    red = jax.ShapeDtypeStruct((2, d // 4, d), F32)
    return (slots, seqs), in_specs, scratch, red, tok


def attn_first(layer, x, dy, w, partial, wup, wdn):
    grid, in_specs, scratch, red, tok = attn_specs(layer, x, w)
    slots, nw, d = w.shape
    gathered = [jax.ShapeDtypeStruct((slots, d, d), BF16)] * 2
    return pl.pallas_call(
        functools.partial(attn_first_kernel, layer),
        out_shape=[jax.ShapeDtypeStruct((d, tok), BF16), jax.ShapeDtypeStruct((slots, 4, d // 4, nw), F32)] + gathered + [red],
        grid=grid,
        in_specs=in_specs + [ANY, ANY],
        out_specs=[whole(d, tok)] + [ANY] * 4,
        scratch_shapes=scratch + [pltpu.VMEM((d, d), BF16)] + SEMS,
        compiler_params=params(2, 2),
        name='attn_first',
    )(x, dy, w, partial, wup, wdn)


def attn_last(layer, x, dy, w, partial):
    grid, in_specs, scratch, red, tok = attn_specs(layer, x, w)
    slots, nw, d = w.shape
    seq = x.shape[2]
    return pl.pallas_call(
        attn_last_kernel,
        out_shape=[jax.ShapeDtypeStruct((x.shape[1], seq, d), BF16), red, jax.ShapeDtypeStruct(red.shape[1:], F32)],
        grid=grid,
        in_specs=in_specs,
        out_specs=[ANY] * 3,
        scratch_shapes=scratch + [pltpu.VMEM((slots, seq, d), BF16), pltpu.SemaphoreType.REGULAR((4,))] + SEMS,
        compiler_params=params(3, 2),
        name='attn_last',
    )(x, dy, w, partial)


def solution(mesh):
    assert dict(mesh.shape) == {'dpy': 2, 'dpx': 2, 'tp': SLOTS}
    act_spec = P(None, DATA_AXES, None, None)

    def device_backward(x_saved, y_saved, dz_top, w_qkv, w_out, w_up, w_down):
        layers, d = w_up.shape[:2]
        assert layers == 2
        heads, hd = w_out.shape[1:3]
        n = 3 * heads * hd
        wq = w_qkv.transpose(0, 2, 3, 4, 1).reshape(layers, n, d)
        wo = w_out.reshape(layers, heads * hd, d)
        dy1, gm1, wa1 = mlp_first(1, y_saved, dz_top, w_up, w_down, wq, wo)
        dx1, ga1, w1_0, w2_0, rm1 = attn_first(1, x_saved, dy1, wa1, gm1, w_up, w_down)
        dy0, gm0, wa0, ra1 = mlp_second(0, y_saved, dx1, w1_0, w2_0, ga1, wq, wo)
        d_input, rm0, ra0 = attn_last(0, x_saved, dy0, wa0, gm0)
        g_a = jnp.stack([ra0, ra1])
        g_qkv = g_a[:, :, :n].reshape(layers, d // 4, 3, heads, hd)
        g_out = g_a[:, :, n:].transpose(0, 2, 1).reshape(layers, heads, hd, d // 4)
        return d_input, g_qkv, g_out, jnp.stack([rm0[1], rm1[1]]), jnp.stack([rm0[0], rm1[0]])

    tp_last = P(None, None, None, 'tp', None), P(None, 'tp', None, None), P(None, None, 'tp'), P(None, 'tp', None)
    return jax.shard_map(device_backward, mesh=mesh,
                         in_specs=(act_spec, act_spec, P(DATA_AXES, None, None)) + tp_last,
                         out_specs=(P(DATA_AXES, None, None), P(None, DATA_AXES, None, 'tp', None), P(None, 'tp', None, DATA_AXES), P(None, DATA_AXES, 'tp'), P(None, ('tp', 'dpy', 'dpx'), None)),
                         check_vma=False)
```

time: 2310 us -> 480 us (0.21)
  waiting for transfers between devices: 1400 us -> 0 us
  matrix products: 720 us -> 0 us
  Pallas kernels: 0 us -> 453 us
  other arithmetic: 114 us -> 4.11 us
  local copies, waits for them, and re-layouts: 46.5 us -> 15 us
    psum x4 -> x0, waiting for transfers between devices: 1400 us -> none  [the longest x2 797 us: layer_backward(): lax.psum(attn_part, 'tp')]
    dot_general x28 -> x0, matrix products: 670 us -> none  [the longest x2 128 us: layer_backward(): jnp.einsum('bhqk,bqhe->bkhe', d_scores, q_heads, preferred_element_type=j...]
    pallas_call x0 -> x4, Pallas kernels: none -> 453 us  [the longest x1 160 us: attn_last(): pl.pallas_call(attn_last_kernel, out_shape=[jax.ShapeDtypeStruct((x.shape...]
    convert_element_type x6 -> x0, other arithmetic: 111 us -> none  [the longest x2 54.8 us: layer_backward(): prob_bf = attn_prob.astype(jnp.bfloat16)]
    sub x2 -> x0, matrix products: 50 us -> none  [layer_backward(): attn_prob = jax.nn.softmax(scores, axis=-1)]
    unnamed x52 -> x5, local copies, waits for them, and re-layouts: 46.5 us -> 10.5 us
  transfers between devices with their start and end apart: 12 -> 0, of which waited for: 5 -> 0; matrix products, arithmetic and copies ran while one was open for 22% -> 0% of each run, Pallas kernels for 0% -> 0%
where the time goes in v3:
time: 480 us; the launch traced here: 473 us
  Pallas kernels  453 us (94%)
  local copies, waits for them, and re-layouts  15 us (3%)
    pallas_call x1, Pallas kernels, attn_last(): pl.pallas_call(attn_last_kernel, out_shape=[jax.ShapeDtypeStruct((x.shape...  160 us
    pallas_call x1, Pallas kernels, attn_first(): pl.pallas_call(functools.partial(attn_first_kernel, layer), out_shape=[ja...  133 us
    pallas_call x1, Pallas kernels, mlp_first(): pl.pallas_call(functools.partial(mlp_first_kernel, layer), out_shape=(jax...  83.4 us
    pallas_call x1, Pallas kernels, mlp_second(): pl.pallas_call(functools.partial(mlp_second_kernel, layer), out_shape=(ja...  76.2 us
    unnamed x5, local copies, waits for them, and re-layouts  10.5 us

profile of v3, /device:TPU:0, one launch (start us, length us, event | category | flops | bytes accessed | tf_op | source)
XLA Modules:
  0.0 472.8 jit_solution(12397313951050932363)
XLA Ops:
  0.6 83.4 %mlp_first.1 = (bf16[768,2048]{1,0:T(8,128)(2,1)}, f32[4,2,4,192,768]{4,3,2,1,0:T(8,128)}, bf16[4,768,768]{2,1,0:T(8,128)(2,1)}) custom-call(bf16[2,16,512,768]{3,2,1,0:T(8,128)(2,1)} %y_ref.3, bf16[16,512,768]{2,1,0:T(8,128)(2,1)} %dz_ref.1, bf16[2,768,768]{2,1,0:T(8,128)(2,1)} %wup.3, bf16[2,768,768]{2,1,0:T(8,128)(2,1)} %wdn.3, ...), custom_call_target="tpu_custom_call" | custom-call | tf_op jit(solution)/shard_map/mlp_first/pallas_call | solution.py:390
  84.0 132.6 %attn_first.1 = (bf16[768,2048]{1,0:T(8,128)(2,1)}, f32[4,4,192,768]{3,2,1,0:T(8,128)}, bf16[4,768,768]{2,1,0:T(8,128)(2,1)}, bf16[4,768,768]{2,1,0:T(8,128)(2,1)}, f32[2,192,768]{2,1,0:T(8,128)}) custom-call(bf16[2,16,512,768]{3,2,1,0:T(8,128)(2,1)} %x_ref.3, bf16[768,2048]{1,0:T(8,128)(2,1)} %get-tuple-element.20.dy_ref, ...), custom_call_target="tpu_custom_call" | custom-call | tf_op jit(solution)/shard_map/attn_first/pallas_call | solution.py:726
  216.6 2.1 fusion.3
  218.7 76.2 %mlp_second.1 = (bf16[768,2048]{1,0:T(8,128)(2,1)}, f32[4,2,4,192,768]{4,3,2,1,0:T(8,128)}, bf16[4,768,768]{2,1,0:T(8,128)(2,1)}, f32[192,768]{1,0:T(8,128)}) custom-call(bf16[2,16,512,768]{3,2,1,0:T(8,128)(2,1)} %y_ref.3, bf16[768,2048]{1,0:T(8,128)(2,1)} %get-tuple-element.23.dz_ref, bf16[4,768,768]{2,1,0:T(8,128)(2,1)} %get-tuple-element.24.w1_ref, ...), custom_call_target="tpu_custom_call" | custom-call | tf_op jit(solution)/shard_map/mlp_second/pallas_call | solution.py:443
  294.9 160.4 %attn_last.1 = (bf16[16,512,768]{2,1,0:T(8,128)(2,1)}, f32[2,192,768]{2,1,0:T(8,128)}, f32[192,768]{1,0:T(8,128)}) custom-call(bf16[2,16,512,768]{3,2,1,0:T(8,128)(2,1)} %x_ref.3, bf16[768,2048]{1,0:T(8,128)(2,1)} %get-tuple-element.27.dy_ref, bf16[4,768,768]{2,1,0:T(8,128)(2,1)} %get-tuple-element.28.w_ref, f32[4,2,4,192,768]{4,3,2,1,0:T(8,128)} %get-tuple-element.29.partial), custom_call_target="tpu_custom_call" | custom-call | tf_op jit(solution)/shard_map/attn_last/pallas_call | solution.py:742
  455.3 1.2 fusion.1
  456.5 0.0 copy-start.1
  456.5 1.3 fusion
  457.9 0.9 copy.15
  458.8 0.0 copy-start
  458.8 1.4 copy.14
  460.2 0.0 copy-done.1
  460.2 0.1 fusion.2
  460.3 0.0 copy-done
  460.3 1.6 pad_maximum_fusion
  461.9 10.5 %copy.17 = bf16[16,512,768]{2,1,0:T(8,128)(2,1)} copy(bf16[16,512,768]{2,1,0:T(8,128)(2,1)} %get-tuple-element.51) | data formatting | bytes 25165824
Async XLA Ops:
  456.5 3.7 copy-start.1
  458.8 1.5 copy-start
